TPU v7x, 16 devices: a 4x2x1 block of a 4x4x8 slice. The times are simulated.
16 devices in a mesh: dp: 2 (over y, z), x: 8 (over x, core).
Axes of the slice: x: 4, y: 2, z: 1, core: 2. Of those that a mesh axis runs over, the one named last changes fastest.
The devices are a block of a 4x4x8 slice.
Arguments:
- c_raw: bfloat16 [96, 6144, 512], P('dp', 'x'), parts along dimension 0
- k_raw: bfloat16 [96, 6144, 64], P('dp', 'x'), parts along dimension 0
- norm_gain: bfloat16 [512], replicated
- rope_cos: float32 [6144, 32], P('x')
- rope_sin: float32 [6144, 32], P('x')
- seq_lens: int32 [96], P('dp'), parts along dimension 0
- q_lat: bfloat16 [96, 128, 512], P(('dp', 'x')), parts along dimension 0
- q_rope: bfloat16 [96, 128, 64], P(('dp', 'x')), parts along dimension 0
Outputs:
- output 1: bfloat16 [96, 6144, 512], P(('dp', 'x')), parts along dimension 0
- output 2: bfloat16 [96, 6144, 64], P(('dp', 'x')), parts along dimension 0
- output 3: bfloat16 [96, 128, 512], P(('dp', 'x')), parts along dimension 0
There are 2 independent parts. A program takes and returns all parts, laid end to end along the dimension named above; an argument that names none is the same for every part.
All inputs are finite; a program needn't handle non-finite values.
Results may differ from a plain program's by a relative error of at most 0.00558648.
Values are sent between devices in bfloat16 or wider.
A program may use at most 768 MiB of HBM per device.

v0:
```python
import jax
import jax.numpy as jnp
from jax import lax
from jax.sharding import PartitionSpec as P

NORM_EPS = 1e-6


def normed_rope(c_raw, k_raw, norm_gain, rope_cos, rope_sin, valid):
    lat_f32 = c_raw.astype(jnp.float32)
    inv_rms = lax.rsqrt(jnp.mean(lat_f32 * lat_f32, axis=-1, keepdims=True) + NORM_EPS)
    c_norm = jnp.where(valid[..., None], lat_f32 * inv_rms * norm_gain.astype(jnp.float32), 0.0)
    half_dim = k_raw.shape[-1] // 2
    key_f32 = k_raw.astype(jnp.float32)
    key_lo = key_f32[..., :half_dim]
    key_hi = key_f32[..., half_dim:]
    rotated = jnp.concatenate([key_lo * rope_cos - key_hi * rope_sin, key_hi * rope_cos + key_lo * rope_sin], axis=-1)
    k_rope = jnp.where(valid[..., None], rotated, 0.0)
    return c_norm.astype(jnp.bfloat16), k_rope.astype(jnp.bfloat16)


def latent_attention(q_lat, q_rope, c_cache, kr_cache, valid):
    attn_scale = (q_lat.shape[-1] + q_rope.shape[-1]) ** -0.5
    scores = jnp.einsum("rhk,rsk->rhs", q_lat, c_cache, preferred_element_type=jnp.float32)
    scores = scores + jnp.einsum("rhe,rse->rhs", q_rope, kr_cache, preferred_element_type=jnp.float32)
    scores = jnp.where(valid[:, None, :], scores * attn_scale, -1e30)
    weights = jnp.exp(scores - jnp.max(scores, axis=-1, keepdims=True))
    weight_sum = jnp.sum(weights, axis=-1)
    weighted = jnp.einsum("rhs,rsk->rhk", weights.astype(jnp.bfloat16), c_cache, preferred_element_type=jnp.float32)
    return (weighted / weight_sum[..., None]).astype(jnp.bfloat16)


def solution(mesh):
    seq_spec = P("dp", "x", None)
    req_spec = P(("dp", "x"), None, None)

    def local_step(c_raw, k_raw, norm_gain, rope_cos, rope_sin, seq_lens, q_lat, q_rope):
        dev_index = lax.axis_index("x")
        seq_local = c_raw.shape[1]
        req_local = q_lat.shape[0]
        positions = dev_index * seq_local + jnp.arange(seq_local)
        valid = positions[None, :] < seq_lens[:, None]
        c_norm, k_rope = normed_rope(c_raw, k_raw, norm_gain, rope_cos, rope_sin, valid)
        c_cache = lax.all_to_all(c_norm, "x", 0, 1, tiled=True)
        kr_cache = lax.all_to_all(k_rope, "x", 0, 1, tiled=True)
        own_lens = lax.dynamic_slice_in_dim(seq_lens, dev_index * req_local, req_local)
        own_valid = jnp.arange(c_cache.shape[1])[None, :] < own_lens[:, None]
        o_lat = latent_attention(q_lat, q_rope, c_cache, kr_cache, own_valid)
        return c_cache, kr_cache, o_lat

    return jax.shard_map(local_step, mesh=mesh, in_specs=(seq_spec, seq_spec, P(None), P("x", None), P("x", None), P("dp"), req_spec, req_spec), out_specs=(req_spec, req_spec, req_spec), check_vma=False)
```

profile of v0, /device:TPU:112, one launch (start us, length us, event | category | flops | bytes accessed | tf_op | source)
XLA Modules:
  0.0 580.7 jit_solution(9959482653025940834)
XLA Ops:
  0.6 0.0 copy-start
  0.7 3.6 convert_element_type.24
  4.3 0.7 broadcast_compare_fusion
  5.1 2.5 multiply_subtract_fusion
  7.6 3.7 fusion.9
  11.3 5.3 all-to-all-start.1
  16.6 0.0 copy-start.4
  16.6 12.6 %fusion = f32[48,768]{1,0:T(8,128)S(1)} fusion(bf16[48,768,512]{2,1,0:T(8,128)(2,1)} %param.8), kind=kLoop, calls=%fused_computation.2 | loop fusion | flops 56586240 | bytes 37896192 | tf_op jit(solution)/shard_map/reduce_sum | solution.py:11
  29.2 0.0 copy-done.4
  29.2 25.3 %fusion.3 = bf16[48,768,512]{2,1,0:T(8,128)(2,1)} fusion(bf16[48,768,512]{2,1,0:T(8,128)(2,1)} %param.8, f32[512]{0:T(512)S(1)} %convert_element_type.22, f32[48,768]{1,0:T(8,128)S(1)} %add_rsqrt_fusion, pred[48,768]{1,0:T(8,128)(4,1)S(1)} %broadcast_compare_fusion), kind=kLoop, calls=%fused_computation.5 | loop fusion | flops 94371840 | bytes 75683840 | tf_op jit(solution)/shard_map/convert_element_type | solution.py:19
  54.6 0.0 copy-start.5
  54.6 17.3 %all-to-all-done.1 = bf16[48,768,64]{1,2,0:T(8,128)(2,1)} async-done(((bf16[48,768,64]{1,2,0:T(8,128)(2,1)}), bf16[48,768,64]{1,2,0:T(8,128)(2,1)}, u32[]{:S(2)}, u32[]{:S(2)}) %all-to-all-start.1) | async-done | bytes 4718624 | tf_op jit(solution)/shard_map/all_to_all | solution.py:45
  71.8 7.8 %all-to-all-start = ((bf16[48,768,512]{2,1,0:T(8,128)(2,1)}), bf16[48,768,512]{2,1,0:T(8,128)(2,1)}, u32[]{:S(2)}, u32[]{:S(2)}) async-start(bf16[48,768,512]{2,1,0:T(8,128)(2,1)} %fusion.3), calls=%async_computation | async-start | bytes 75497472 | tf_op jit(solution)/shard_map/all_to_all | solution.py:44
  79.7 0.0 copy-done.5
  79.7 0.1 dynamic_slice.3
  79.7 0.1 iota_compare_fusion
  79.8 7.3 %copy.16 = bf16[8,6,768,64]{2,0,3,1:T(8,128)(2,1)} copy(bf16[8,6,768,64]{2,3,1,0:T(8,128)(2,1)} %bitcast.3) | data formatting | bytes 9437184 | tf_op jit(solution)/shard_map/all_to_all | solution.py:45
  87.1 7.7 %all_to_all.33 = bf16[6,6144,64]{1,2,0:T(8,128)(2,1)} reshape(bf16[6,8,768,64]{2,1,3,0:T(8,128)(2,1)} %bitcast.32) | data formatting | bytes 9437184 | tf_op jit(solution)/shard_map/all_to_all | solution.py:45
  94.8 393.6 %all-to-all-done = bf16[48,768,512]{2,1,0:T(8,128)(2,1)} async-done(((bf16[48,768,512]{2,1,0:T(8,128)(2,1)}), bf16[48,768,512]{2,1,0:T(8,128)(2,1)}, u32[]{:S(2)}, u32[]{:S(2)}) %all-to-all-start) | async-done | bytes 37748768 | tf_op jit(solution)/shard_map/all_to_all | solution.py:44
  488.4 25.4 %copy.11 = bf16[8,6,768,512]{3,2,0,1:T(8,128)(2,1)} copy(bf16[8,6,768,512]{3,2,1,0:T(8,128)(2,1)} %bitcast) | data formatting | bytes 75497472 | tf_op jit(solution)/shard_map/all_to_all | solution.py:44
  513.9 0.0 copy-done
  513.9 0.0 copy-start.2
  513.9 0.0 copy-start.3
  513.9 23.8 %fusion.13 = f32[6,6144,128]{2,1,0:T(8,128)} fusion(bf16[6,6144,512]{2,1,0:T(8,128)(2,1)} %bitcast.29, bf16[6,128,512]{2,1,0:T(8,128)(2,1)S(1)} %copy-done), kind=kOutput, calls=%fused_computation.24 | convolution fusion | flops 4831838208 | bytes 57409536 | tf_op jit(solution)/shard_map/rhk,rsk->rhs/dot_general | solution.py:24
  537.6 0.0 copy-done.2
  537.6 0.0 copy-done.3
  537.6 13.5 %bitcast_reduce_fusion = (f32[6,128]{1,0:T(8,128)S(1)}, f32[6,6144,128]{2,1,0:T(8,128)}) fusion(f32[6,6144,128]{2,1,0:T(8,128)} %fusion.13, bf16[6,6144,64]{1,2,0:T(8,128)(2,1)S(1)} %copy-done.2, bf16[6,128,64]{1,2,0:T(8,128)(2,1)S(1)} %copy-done.3, pred[6,6144]{1,0:T(8,128)(4,1)S(1)} %iota_compare_fusion), kind=kOutput, calls=%fused_computation.7 | convolution fusion | flops 622853376 | bytes 42605568 | tf_op jit(solution)/shard_map/rhe,rse->rhs/dot_general | solution.py:25
  551.1 8.8 %fusion.5 = f32[6,128]{1,0:T(8,128)S(1)} fusion(f32[6,6144,128]{2,1,0:T(8,128)} %get-tuple-element.6, f32[6,128]{1,0:T(8,128)S(1)} %get-tuple-element.5), kind=kLoop, calls=%fused_computation.10 | loop fusion | flops 9436416 | bytes 18880512 | tf_op jit(solution)/shard_map/reduce_sum | solution.py:28
  560.0 0.0 copy-start.1
  560.0 20.7 %divide_convert_fusion = bf16[6,128,512]{2,1,0:T(8,128)(2,1)} fusion(bf16[6,6144,512]{2,1,0:T(8,128)(2,1)} %bitcast.30, f32[6,6144,128]{2,1,0:T(8,128)} %get-tuple-element.6, f32[6,128]{1,0:T(8,128)S(1)} %get-tuple-element.5, f32[6,128]{1,0:T(8,128)S(1)} %fusion.5), kind=kOutput, calls=%fused_computation.19 | convolution fusion | flops 4842061824 | bytes 57415680 | tf_op jit(solution)/shard_map/rhs,rsk->rhk/dot_general | solution.py:29
  580.7 0.0 copy-done.1
  (3 shorter events, 0.0 us)
Async XLA Ops:
  0.6 513.2 %copy-start = (bf16[6,128,512]{2,1,0:T(8,128)(2,1)S(1)}, bf16[6,128,512]{2,1,0:T(8,128)(2,1)}, u32[]{:S(2)}) copy-start(bf16[6,128,512]{2,1,0:T(8,128)(2,1)} %param.14) | copy-start | bytes 2359300
  11.3 60.6 %all-to-all-start.1 = ((bf16[48,768,64]{1,2,0:T(8,128)(2,1)}), bf16[48,768,64]{1,2,0:T(8,128)(2,1)}, u32[]{:S(2)}, u32[]{:S(2)}) async-start(bf16[48,768,64]{1,2,0:T(8,128)(2,1)} %fusion.9), calls=%async_computation.1 | async-start | bytes 9437184 | tf_op jit(solution)/shard_map/all_to_all | solution.py:45
  16.6 12.6 %copy-start.4 = (bf16[512]{0:T(512)(128)(2,1)S(1)}, bf16[512]{0:T(512)(128)(2,1)}, u32[]{:S(2)}) copy-start(bf16[512]{0:T(512)(128)(2,1)} %param.10) | copy-start | bytes 3076
  54.6 25.1 %copy-start.5 = (s32[48]{0:T(128)S(1)}, s32[48]{0:T(128)}, u32[]{:S(2)}) copy-start(s32[48]{0:T(128)} %param.13) | copy-start | bytes 580
  71.8 416.6 %all-to-all-start = ((bf16[48,768,512]{2,1,0:T(8,128)(2,1)}), bf16[48,768,512]{2,1,0:T(8,128)(2,1)}, u32[]{:S(2)}, u32[]{:S(2)}) async-start(bf16[48,768,512]{2,1,0:T(8,128)(2,1)} %fusion.3), calls=%async_computation | async-start | bytes 75497472 | tf_op jit(solution)/shard_map/all_to_all | solution.py:44
  513.9 23.8 %copy-start.2 = (bf16[6,6144,64]{1,2,0:T(8,128)(2,1)S(1)}, bf16[6,6144,64]{1,2,0:T(8,128)(2,1)}, u32[]{:S(2)}) copy-start(bf16[6,6144,64]{1,2,0:T(8,128)(2,1)} %all_to_all.33) | copy-start | bytes 14155780
  513.9 23.8 %copy-start.3 = (bf16[6,128,64]{1,2,0:T(8,128)(2,1)S(1)}, bf16[6,128,64]{1,2,0:T(8,128)(2,1)}, u32[]{:S(2)}) copy-start(bf16[6,128,64]{1,2,0:T(8,128)(2,1)} %param.15) | copy-start | bytes 294916
  560.0 20.7 %copy-start.1 = (bf16[6,128,512]{2,1,0:T(8,128)(2,1)S(1)}, bf16[6,128,512]{2,1,0:T(8,128)(2,1)}, u32[]{:S(2)}) copy-start(bf16[6,128,512]{2,1,0:T(8,128)(2,1)} %param.14) | copy-start | bytes 2359300
where the time goes:
time: 581 us
  waiting for transfers between devices  411 us (71%)
  matrix products  58 us (10%)
  other arithmetic  57.5 us (10%)
  local copies, waits for them, and re-layouts  40.5 us (7%)
  starting transfers between devices  13.1 us (2%)
    all_to_all x1, waiting for transfers between devices, local_step(): c_cache = lax.all_to_all(c_norm, 'x', 0, 1, tiled=True)  394 us
    convert_element_type x2, other arithmetic, normed_rope(): return (c_norm.astype(jnp.bfloat16), k_rope.astype(jnp.bfloat16))  29.1 us
    all_to_all x1, local copies, waits for them, and re-layouts, local_step(): c_cache = lax.all_to_all(c_norm, 'x', 0, 1, tiled=True)  25.4 us
    dot_general x1, matrix products, latent_attention(): jnp.einsum('rhk,rsk->rhs', q_lat, c_cache, preferred_element_type=jnp.flo...  23.8 us
    dot_general x1, matrix products, latent_attention(): jnp.einsum('rhs,rsk->rhk', weights.astype(jnp.bfloat16), c_cache, preferr...  20.7 us
    all_to_all x1, waiting for transfers between devices, local_step(): kr_cache = lax.all_to_all(k_rope, 'x', 0, 1, tiled=True)  17.3 us
    all_to_all x2, local copies, waits for them, and re-layouts, local_step(): kr_cache = lax.all_to_all(k_rope, 'x', 0, 1, tiled=True)  15 us
    dot_general x1, matrix products, latent_attention(): jnp.einsum('rhe,rse->rhs', q_rope, kr_cache, preferred_element_type=jnp.f...  13.5 us
  transfers between devices with their start and end apart: 2, of which 2 were waited for; matrix products, arithmetic and copies ran while one was open for 8% of the time, Pallas kernels for 0%

commit v1 on v0

v1 whole, which is shorter than its diff:
```python
import functools

import jax
import jax.numpy as jnp
from jax import lax
from jax.experimental import pallas as pl
from jax.experimental.pallas import tpu as pltpu
from jax.sharding import PartitionSpec as P

NORM_EPS = 1e-6
CHUNKS = (1, 2, 2, 1)
VMEM_BYTES = 60 * 1024 * 1024


def pack_kernel(first, req_local, lens_ref, c_ref, k_ref, gain_ref, cos_ref, sin_ref, out_ref):
    rows, rank = c_ref.shape[1:]
    length = lens_ref[pl.program_id(0) * req_local + first + pl.program_id(1)]
    left = length - lax.axis_index("x") * rows

    @pl.when(left <= 0)
    def _():
        out_ref[...] = jnp.zeros_like(out_ref)

    @pl.when(left > 0)
    def _():
        lat = c_ref[0].astype(jnp.float32)
        inv = lax.rsqrt(jnp.mean(lat * lat, axis=-1, keepdims=True) + NORM_EPS)
        normed = lat * inv * gain_ref[...].astype(jnp.float32)
        valid = lax.broadcasted_iota(jnp.int32, (rows, 1), 0) < left
        out_ref[0, 0, :rows, :] = jnp.where(valid, normed, 0.0).astype(jnp.bfloat16)
        key = k_ref[0].astype(jnp.float32)
        half = key.shape[0] // 2
        lo, hi = key[:half], key[half:]
        cos, sin = cos_ref[...], sin_ref[...]
        valid = lax.broadcasted_iota(jnp.int32, (1, rows), 1) < left
        store_rope(out_ref, 0, jnp.where(valid, lo * cos - hi * sin, 0.0).astype(jnp.bfloat16), rows, rank)
        store_rope(out_ref, half, jnp.where(valid, hi * cos + lo * sin, 0.0).astype(jnp.bfloat16), rows, rank)


def store_rope(out_ref, at, keys, rows, rank):
    half = keys.shape[0]
    rest = rows - rank
    side = (at // half) * rest
    out_ref[0, 0, rows + at : rows + at + half, :] = keys[:, :rank]
    out_ref[0, 0, rows + 2 * half : rows + 3 * half, side : side + rest] = keys[:, rank:]


def load_rope(land_ref, kr_ref, rows, rank):
    half = kr_ref.shape[1] // 2
    rest = rows - rank
    kr_ref[0, :, :rank] = land_ref[0, 0, rows : rows + 2 * half, :]
    for at in (0, 1):
        kr_ref[0, at * half : (at + 1) * half, rank:] = land_ref[0, 0, rows + 2 * half : rows + 3 * half, at * rest : (at + 1) * rest]


def pack(lens, c_raw, k_raw, gain, cos, sin, n, req_local, first, count):
    requests, rows, rank = c_raw.shape
    width = k_raw.shape[1]
    total = rows + rows * width // rank
    req = lambda d, m, *_: (d * req_local + first + m, 0, 0)
    fixed = lambda d, m, *_: (0, 0)
    return pl.pallas_call(
        functools.partial(pack_kernel, first, req_local),
        grid_spec=pltpu.PrefetchScalarGridSpec(
            num_scalar_prefetch=1,
            grid=(n, count),
            in_specs=[
                pl.BlockSpec((1, rows, rank), req),
                pl.BlockSpec((1, width, rows), req),
                pl.BlockSpec((1, rank), fixed),
                pl.BlockSpec((width // 2, rows), fixed),
                pl.BlockSpec((width // 2, rows), fixed),
            ],
            out_specs=pl.BlockSpec((1, 1, total, rank), lambda d, m, *_: (d, m, 0, 0)),
        ),
        out_shape=jax.ShapeDtypeStruct((n, count, total, rank), jnp.bfloat16),
        compiler_params=pltpu.CompilerParams(vmem_limit_bytes=VMEM_BYTES),
        cost_estimate=pl.CostEstimate(flops=n * count * rows * rank * 100, bytes_accessed=n * count * total * rank * 4, transcendentals=0),
        name=f"pack_{first}",
    )(lens, c_raw, k_raw, gain, cos, sin)


def attend_kernel(n, scale, lens_ref, land_ref, qa_ref, qr_ref, *rest):
    c_out, kr_out, o_out, m_scr, l_scr, acc_scr = rest[-6:]
    slot, blk = pl.program_id(0), pl.program_id(1)
    rows, rank = c_out.shape[1:]
    length = lens_ref[slot]

    @pl.when(blk == 0)
    def _():
        m_scr[...] = jnp.full_like(m_scr, -1e30)
        l_scr[...] = jnp.zeros_like(l_scr)
        acc_scr[...] = jnp.zeros_like(acc_scr)

    @pl.when(blk * rows >= length)
    def _():
        c_out[...] = jnp.zeros_like(c_out)
        kr_out[...] = jnp.zeros_like(kr_out)

    @pl.when(blk * rows < length)
    def _():
        lat = land_ref[0, 0, :rows, :]
        c_out[0] = lat
        load_rope(land_ref, kr_out, rows, rank)
        contract = (((1,), (1,)), ((), ()))
        s = lax.dot_general(qa_ref[0], lat, contract, preferred_element_type=jnp.float32)
        s = s + jnp.dot(qr_ref[0], kr_out[0], preferred_element_type=jnp.float32)
        pos = blk * rows + lax.broadcasted_iota(jnp.int32, (1, rows), 1)
        s = jnp.where(pos < length, s * scale, -1e30)
        m_old = m_scr[...]
        m_new = jnp.maximum(m_old, jnp.max(s, axis=-1, keepdims=True))
        alpha = jnp.exp(m_old - m_new)
        p = jnp.exp(s - m_new)
        l_scr[...] = l_scr[...] * alpha + jnp.sum(p, axis=-1, keepdims=True)
        m_scr[...] = m_new
        acc_scr[...] = acc_scr[...] * alpha + lax.dot_general(
            p.astype(jnp.bfloat16), lat, (((1,), (0,)), ((), ())), preferred_element_type=jnp.float32)

    @pl.when(blk == n - 1)
    def _():
        o_out[0] = (acc_scr[...] / l_scr[...]).astype(jnp.bfloat16)


def attend(own_lens, landed, q_lat, q_rope, prev, n, rows, first, count):
    req_local, heads, rank = q_lat.shape
    width = q_rope.shape[2]
    total = landed.shape[2]
    scale = (rank + width) ** -0.5
    outs = [
        jax.ShapeDtypeStruct((req_local, n * rows, rank), jnp.bfloat16),
        jax.ShapeDtypeStruct((req_local, width, n * rows), jnp.bfloat16),
        jax.ShapeDtypeStruct((req_local, heads, rank), jnp.bfloat16),
    ]
    land = lambda m, i, lens: (jnp.minimum(i, (lens[m] - 1) // rows), m, 0, 0)
    slot = lambda m, i, lens: (first + m, 0, 0)
    any_spec = pl.BlockSpec(memory_space=pl.ANY)
    prev = list(prev) if prev is not None else []
    return pl.pallas_call(
        functools.partial(attend_kernel, n, scale),
        grid_spec=pltpu.PrefetchScalarGridSpec(
            num_scalar_prefetch=1,
            grid=(count, n),
            in_specs=[
                pl.BlockSpec((1, 1, total, rank), land),
                pl.BlockSpec((1, heads, rank), slot),
                pl.BlockSpec((1, heads, width), slot),
            ] + [any_spec] * len(prev),
            out_specs=[
                pl.BlockSpec((1, rows, rank), lambda m, i, lens: (first + m, i, 0)),
                pl.BlockSpec((1, width, rows), lambda m, i, lens: (first + m, 0, i)),
                pl.BlockSpec((1, heads, rank), slot),
            ],
            scratch_shapes=[
                pltpu.VMEM((heads, 1), jnp.float32),
                pltpu.VMEM((heads, 1), jnp.float32),
                pltpu.VMEM((heads, rank), jnp.float32),
            ],
        ),
        out_shape=outs,
        input_output_aliases={4 + k: k for k in range(len(prev))},
        compiler_params=pltpu.CompilerParams(vmem_limit_bytes=VMEM_BYTES),
        cost_estimate=pl.CostEstimate(flops=count * n * rows * heads * (2 * rank + width) * 2, bytes_accessed=count * n * rows * rank * 4, transcendentals=0),
        name=f"attend_{first}",
    )(own_lens[first : first + count], landed, q_lat, q_rope, *prev)


def solution(mesh):
    seq_spec = P("dp", "x", None)
    req_spec = P(("dp", "x"), None, None)
    n = mesh.shape["x"]

    def local_step(c_raw, k_raw, norm_gain, rope_cos, rope_sin, seq_lens, q_lat, q_rope):
        rows = c_raw.shape[1]
        req_local = q_lat.shape[0]
        own_lens = lax.dynamic_slice_in_dim(seq_lens, lax.axis_index("x") * req_local, req_local)
        k_raw = jnp.swapaxes(k_raw, 1, 2)
        tables = (norm_gain[None, :], rope_cos.T, rope_sin.T)
        landed, first = [], 0
        for count in CHUNKS:
            packed = pack(seq_lens, c_raw, k_raw, *tables, n, req_local, first, count)
            landed.append((first, count, lax.all_to_all(packed, "x", 0, 0, tiled=True)))
            first += count
        outs = None
        for first, count, block in landed:
            outs = attend(own_lens, block, q_lat, q_rope, outs, n, rows, first, count)
        return outs[0], jnp.swapaxes(outs[1], 1, 2), outs[2]

    return jax.shard_map(local_step, mesh=mesh, in_specs=(seq_spec, seq_spec, P(None), P("x", None), P("x", None), P("dp"), req_spec, req_spec), out_specs=(req_spec, req_spec, req_spec), check_vma=False)
```

time: 581 us -> 520 us (0.90)
  Pallas kernels: 0 us -> 110 us
  matrix products: 58 us -> 0 us
  other arithmetic: 57.5 us -> 0 us
  local copies, waits for them, and re-layouts: 40.5 us -> 3.43 us
  waiting for transfers between devices: 411 us -> 380 us
  starting transfers between devices: 13.1 us -> 21.4 us
    pallas_call x0 -> x8, Pallas kernels: none -> 110 us  [the longest x4 57.5 us: pack(): pl.pallas_call(functools.partial(pack_kernel, first, req_local), grid_spe...]
    dot_general x3 -> x0, matrix products: 58 us -> none  [the longest x1 23.8 us: latent_attention(): jnp.einsum('rhk,rsk->rhs', q_lat, c_cache, preferred_element_type=jnp.flo...]
    all_to_all x3 -> x0, local copies, waits for them, and re-layouts: 40.4 us -> none  [the longest x1 25.4 us: local_step(): c_cache = lax.all_to_all(c_norm, 'x', 0, 1, tiled=True)]
    convert_element_type x4 -> x0, other arithmetic: 32.7 us -> none  [the longest x2 29.1 us: normed_rope(): return (c_norm.astype(jnp.bfloat16), k_rope.astype(jnp.bfloat16))]
    all_to_all x2 -> x4, waiting for transfers between devices: 411 us -> 380 us  [local_step(): landed.append((first, count, lax.all_to_all(packed, 'x', 0, 0, tiled=True)))]
    reduce_sum x2 -> x0, other arithmetic: 21.4 us -> none  [the longest x1 12.6 us: normed_rope(): jnp.mean(lat_f32 * lat_f32, axis=-1, keepdims=True) + NORM_EPS]
    all_to_all x2 -> x4, starting transfers between devices: 13.1 us -> 21.4 us  [local_step(): landed.append((first, count, lax.all_to_all(packed, 'x', 0, 0, tiled=True)))]
  transfers between devices with their start and end apart: 2 -> 4, of which waited for: 2 -> 4; matrix products, arithmetic and copies ran while one was open for 8% -> 0% of each run, Pallas kernels for 0% -> 18%
where the time goes in v1:
time: 520 us; the launch traced here: 516 us
  waiting for transfers between devices  380 us (73%)
  Pallas kernels  110 us (21%)
  starting transfers between devices  21.4 us (4%)
    all_to_all x4, waiting for transfers between devices, local_step(): landed.append((first, count, lax.all_to_all(packed, 'x', 0, 0, tiled=True)))  380 us
    pallas_call x4, Pallas kernels, pack(): pl.pallas_call(functools.partial(pack_kernel, first, req_local), grid_spe...  57.5 us
    pallas_call x4, Pallas kernels, attend(): pl.pallas_call(functools.partial(attend_kernel, n, scale), grid_spec=pltp...  52.9 us
    all_to_all x4, starting transfers between devices, local_step(): landed.append((first, count, lax.all_to_all(packed, 'x', 0, 0, tiled=True)))  21.4 us
  transfers between devices with their start and end apart: 4, of which 4 were waited for; matrix products, arithmetic and copies ran while one was open for 0% of the time, Pallas kernels for 18%

profile of v1, /device:TPU:112, one launch (start us, length us, event | category | flops | bytes accessed | tf_op | source)
XLA Modules:
  0.0 515.8 jit_solution(3661638221443126399)
XLA Ops:
  0.6 1.3 broadcast_in_dim.3.gain_ref
  1.9 10.2 %pack_0.1 = bf16[8,1,864,512]{3,2,1,0:T(8,128)(2,1)} custom-call(s32[48]{0:T(128)} %lens_ref.7, bf16[48,768,512]{2,1,0:T(8,128)(2,1)} %c_ref.7, bf16[48,64,768]{2,1,0:T(8,128)(2,1)} %bitcast.4, bf16[1,512]{1,0:T(2,128)(2,1)} %broadcast_in_dim.3.gain_ref, f32[32,768]{1,0:T(8,128)} %bitcast.9, f32[32,768]{1,0:T(8,128)} %bitcast.13), custom_call_target="tpu_custom_call" | custom-call | flops 314572800 | bytes 14155776 | tf_op jit(solution)/shard_map/pack_0/pallas_call | solution.py:62
  12.0 5.0 all-to-all-start.3
  17.1 18.6 %pack_1.1 = bf16[8,2,864,512]{3,2,1,0:T(8,128)(2,1)} custom-call(s32[48]{0:T(128)} %lens_ref.7, bf16[48,768,512]{2,1,0:T(8,128)(2,1)} %c_ref.7, bf16[48,64,768]{2,1,0:T(8,128)(2,1)} %bitcast.5, bf16[1,512]{1,0:T(2,128)(2,1)} %broadcast_in_dim.3.gain_ref, f32[32,768]{1,0:T(8,128)} %bitcast.10, f32[32,768]{1,0:T(8,128)} %bitcast.14), custom_call_target="tpu_custom_call" | custom-call | flops 629145600 | bytes 28311552 | tf_op jit(solution)/shard_map/pack_1/pallas_call | solution.py:62
  35.7 61.7 %all-to-all-done.3.land_ref = bf16[8,1,864,512]{3,2,1,0:T(8,128)(2,1)} async-done(((bf16[8,1,864,512]{3,2,1,0:T(8,128)(2,1)}), bf16[8,1,864,512]{3,2,1,0:T(8,128)(2,1)}, u32[]{:S(2)}, u32[]{:S(2)}) %all-to-all-start.3) | async-done | bytes 7077920 | tf_op jit(solution)/shard_map/all_to_all | solution.py:181
  97.4 5.7 %all-to-all-start.2 = ((bf16[8,2,864,512]{3,2,1,0:T(8,128)(2,1)}), bf16[8,2,864,512]{3,2,1,0:T(8,128)(2,1)}, u32[]{:S(2)}, u32[]{:S(2)}) async-start(bf16[8,2,864,512]{3,2,1,0:T(8,128)(2,1)} %pack_1.1), calls=%async_computation.2 | async-start | bytes 28311552 | tf_op jit(solution)/shard_map/all_to_all | solution.py:181
  103.1 18.6 %pack_3.1 = bf16[8,2,864,512]{3,2,1,0:T(8,128)(2,1)} custom-call(s32[48]{0:T(128)} %lens_ref.7, bf16[48,768,512]{2,1,0:T(8,128)(2,1)} %c_ref.7, bf16[48,64,768]{2,1,0:T(8,128)(2,1)} %bitcast.6, bf16[1,512]{1,0:T(2,128)(2,1)} %broadcast_in_dim.3.gain_ref, f32[32,768]{1,0:T(8,128)} %bitcast.11, f32[32,768]{1,0:T(8,128)} %bitcast.15), custom_call_target="tpu_custom_call" | custom-call | flops 629145600 | bytes 28311552 | tf_op jit(solution)/shard_map/pack_3/pallas_call | solution.py:62
  121.7 137.6 %all-to-all-done.2.land_ref = bf16[8,2,864,512]{3,2,1,0:T(8,128)(2,1)} async-done(((bf16[8,2,864,512]{3,2,1,0:T(8,128)(2,1)}), bf16[8,2,864,512]{3,2,1,0:T(8,128)(2,1)}, u32[]{:S(2)}, u32[]{:S(2)}) %all-to-all-start.2) | async-done | bytes 14155808 | tf_op jit(solution)/shard_map/all_to_all | solution.py:181
  259.3 5.7 %all-to-all-start.1 = ((bf16[8,2,864,512]{3,2,1,0:T(8,128)(2,1)}), bf16[8,2,864,512]{3,2,1,0:T(8,128)(2,1)}, u32[]{:S(2)}, u32[]{:S(2)}) async-start(bf16[8,2,864,512]{3,2,1,0:T(8,128)(2,1)} %pack_3.1), calls=%async_computation.1 | async-start | bytes 28311552 | tf_op jit(solution)/shard_map/all_to_all | solution.py:181
  265.0 10.2 %pack_5.1 = bf16[8,1,864,512]{3,2,1,0:T(8,128)(2,1)} custom-call(s32[48]{0:T(128)} %lens_ref.7, bf16[48,768,512]{2,1,0:T(8,128)(2,1)} %c_ref.7, bf16[48,64,768]{2,1,0:T(8,128)(2,1)} %bitcast.7, bf16[1,512]{1,0:T(2,128)(2,1)} %broadcast_in_dim.3.gain_ref, f32[32,768]{1,0:T(8,128)} %bitcast.12, f32[32,768]{1,0:T(8,128)} %bitcast.16), custom_call_target="tpu_custom_call" | custom-call | flops 314572800 | bytes 14155776 | tf_op jit(solution)/shard_map/pack_5/pallas_call | solution.py:62
  275.2 0.0 copy-start.1
  275.2 0.0 copy-start
  275.2 146.0 %all-to-all-done.1.land_ref = bf16[8,2,864,512]{3,2,1,0:T(8,128)(2,1)} async-done(((bf16[8,2,864,512]{3,2,1,0:T(8,128)(2,1)}), bf16[8,2,864,512]{3,2,1,0:T(8,128)(2,1)}, u32[]{:S(2)}, u32[]{:S(2)}) %all-to-all-start.1) | async-done | bytes 14155808 | tf_op jit(solution)/shard_map/all_to_all | solution.py:181
  421.1 5.0 all-to-all-start
  426.2 0.0 copy-done.1
  426.2 0.1 dynamic_slice.3
  426.3 0.0 copy-done
  426.3 0.8 copy.23.qr_ref
  427.1 0.6 fusion
  427.8 0.6 fusion.1
  428.4 8.5 %attend_0.1 = (bf16[6,6144,512]{2,1,0:T(8,128)(2,1)}, bf16[6,64,6144]{2,1,0:T(8,128)(2,1)}, bf16[6,128,512]{2,1,0:T(8,128)(2,1)}) custom-call(s32[1]{0:T(128)} %get-tuple-element.27.lens_ref, bf16[8,1,864,512]{3,2,1,0:T(8,128)(2,1)} %all-to-all-done.3.land_ref, bf16[6,128,512]{2,1,0:T(8,128)(2,1)} %qa_ref.7, bf16[6,128,64]{2,1,0:T(8,128)(2,1)} %copy.23.qr_ref), custom_call_target="tpu_custom_call" | custom-call | flops 1711276032 | bytes 12582912 | tf_op jit(solution)/shard_map/attend_0/pallas_call | solution.py:138
  436.9 18.3 %attend_1.1 = (bf16[6,6144,512]{2,1,0:T(8,128)(2,1)}, bf16[6,64,6144]{2,1,0:T(8,128)(2,1)}, bf16[6,128,512]{2,1,0:T(8,128)(2,1)}) custom-call(s32[2]{0:T(128)} %get-tuple-element.29.lens_ref, bf16[8,2,864,512]{3,2,1,0:T(8,128)(2,1)} %all-to-all-done.2.land_ref, ...), custom_call_target="tpu_custom_call", output_to_operand_aliasing={{0}: (4, {}), {1}: (5, {}), {2}: (6, {})} | custom-call | flops 3422552064 | bytes 25165824 | tf_op jit(solution)/shard_map/attend_1/pallas_call | solution.py:138
  455.2 16.7 %attend_3.1 = (bf16[6,6144,512]{2,1,0:T(8,128)(2,1)}, bf16[6,64,6144]{2,1,0:T(8,128)(2,1)}, bf16[6,128,512]{2,1,0:T(8,128)(2,1)}) custom-call(s32[2]{0:T(128)} %get-tuple-element.30.lens_ref, bf16[8,2,864,512]{3,2,1,0:T(8,128)(2,1)} %all-to-all-done.1.land_ref, ...), custom_call_target="tpu_custom_call", output_to_operand_aliasing={{0}: (4, {}), {1}: (5, {}), {2}: (6, {})} | custom-call | flops 3422552064 | bytes 25165824 | tf_op jit(solution)/shard_map/attend_3/pallas_call | solution.py:138
  471.9 34.6 %all-to-all-done.land_ref = bf16[8,1,864,512]{3,2,1,0:T(8,128)(2,1)} async-done(((bf16[8,1,864,512]{3,2,1,0:T(8,128)(2,1)}), bf16[8,1,864,512]{3,2,1,0:T(8,128)(2,1)}, u32[]{:S(2)}, u32[]{:S(2)}) %all-to-all-start) | async-done | bytes 7077920 | tf_op jit(solution)/shard_map/all_to_all | solution.py:181
  506.5 9.3 %attend_5.1 = (bf16[6,6144,512]{2,1,0:T(8,128)(2,1)}, bf16[6,64,6144]{2,1,0:T(8,128)(2,1)}, bf16[6,128,512]{2,1,0:T(8,128)(2,1)}) custom-call(s32[1]{0:T(128)} %get-tuple-element.28.lens_ref, bf16[8,1,864,512]{3,2,1,0:T(8,128)(2,1)} %all-to-all-done.land_ref, ...), custom_call_target="tpu_custom_call", output_to_operand_aliasing={{0}: (4, {}), {1}: (5, {}), {2}: (6, {})} | custom-call | flops 1711276032 | bytes 12582912 | tf_op jit(solution)/shard_map/attend_5/pallas_call | solution.py:138
Async XLA Ops:
  12.0 85.4 %all-to-all-start.3 = ((bf16[8,1,864,512]{3,2,1,0:T(8,128)(2,1)}), bf16[8,1,864,512]{3,2,1,0:T(8,128)(2,1)}, u32[]{:S(2)}, u32[]{:S(2)}) async-start(bf16[8,1,864,512]{3,2,1,0:T(8,128)(2,1)} %pack_0.1), calls=%async_computation.3 | async-start | bytes 14155776 | tf_op jit(solution)/shard_map/all_to_all | solution.py:181
  97.4 161.9 %all-to-all-start.2 = ((bf16[8,2,864,512]{3,2,1,0:T(8,128)(2,1)}), bf16[8,2,864,512]{3,2,1,0:T(8,128)(2,1)}, u32[]{:S(2)}, u32[]{:S(2)}) async-start(bf16[8,2,864,512]{3,2,1,0:T(8,128)(2,1)} %pack_1.1), calls=%async_computation.2 | async-start | bytes 28311552 | tf_op jit(solution)/shard_map/all_to_all | solution.py:181
  259.3 161.9 %all-to-all-start.1 = ((bf16[8,2,864,512]{3,2,1,0:T(8,128)(2,1)}), bf16[8,2,864,512]{3,2,1,0:T(8,128)(2,1)}, u32[]{:S(2)}, u32[]{:S(2)}) async-start(bf16[8,2,864,512]{3,2,1,0:T(8,128)(2,1)} %pack_3.1), calls=%async_computation.1 | async-start | bytes 28311552 | tf_op jit(solution)/shard_map/all_to_all | solution.py:181
  275.2 151.0 %copy-start.1 = (s32[48]{0:T(128)S(1)}, s32[48]{0:T(128)}, u32[]{:S(2)}) copy-start(s32[48]{0:T(128)} %lens_ref.7) | copy-start | bytes 580
  275.2 151.1 %copy-start = (bf16[6,128,64]{1,2,0:T(8,128)(2,1)S(1)}, bf16[6,128,64]{1,2,0:T(8,128)(2,1)}, u32[]{:S(2)}) copy-start(bf16[6,128,64]{1,2,0:T(8,128)(2,1)} %param.15) | copy-start | bytes 294916
  421.1 85.4 %all-to-all-start = ((bf16[8,1,864,512]{3,2,1,0:T(8,128)(2,1)}), bf16[8,1,864,512]{3,2,1,0:T(8,128)(2,1)}, u32[]{:S(2)}, u32[]{:S(2)}) async-start(bf16[8,1,864,512]{3,2,1,0:T(8,128)(2,1)} %pack_5.1), calls=%async_computation | async-start | bytes 14155776 | tf_op jit(solution)/shard_map/all_to_all | solution.py:181

commit v2 on v1

--- a/solution.py
+++ b/solution.py
@@ -8,41 +8,140 @@
 from jax.sharding import PartitionSpec as P
 
 NORM_EPS = 1e-6
-CHUNKS = (1, 2, 2, 1)
+TAIL = 1
+DEPTH = 3
+STRIPE = 128
 VMEM_BYTES = 60 * 1024 * 1024
 
 
-def pack_kernel(first, req_local, lens_ref, c_ref, k_ref, gain_ref, cos_ref, sin_ref, out_ref):
-    rows, rank = c_ref.shape[1:]
-    length = lens_ref[pl.program_id(0) * req_local + first + pl.program_id(1)]
-    left = length - lax.axis_index("x") * rows
-
-    @pl.when(left <= 0)
-    def _():
-        out_ref[...] = jnp.zeros_like(out_ref)
-
-    @pl.when(left > 0)
-    def _():
-        lat = c_ref[0].astype(jnp.float32)
-        inv = lax.rsqrt(jnp.mean(lat * lat, axis=-1, keepdims=True) + NORM_EPS)
-        normed = lat * inv * gain_ref[...].astype(jnp.float32)
-        valid = lax.broadcasted_iota(jnp.int32, (rows, 1), 0) < left
-        out_ref[0, 0, :rows, :] = jnp.where(valid, normed, 0.0).astype(jnp.bfloat16)
-        key = k_ref[0].astype(jnp.float32)
+def peer(j, n):
+    me = lax.axis_index("x")
+    chip, core = me // 2, me % 2
+    far = j % 3
+    hop = (1 - j // (n - 2)) * (1 + 2 * far - 3 * (far // 2))
+    other = (j // 3) % 2 * (1 - j // (n - 2)) + (j // (n - 2)) * (1 - j % (n - 2))
+    chips = n // 2
+    return (chip + hop) % chips * 2 + (core + other) % 2
+
+
+def send_kernel(n, req_local, tail, lens_ref, c_hbm, k_hbm, gain_ref, cos_ref, sin_ref, land_ref, rest_ref,
+                c_buf, k_buf, out_buf, c_sem, k_sem, send_sem, recv_sem):
+    me = lax.axis_index("x")
+    early = req_local - tail
+    steps = req_local * n
+    depth = out_buf.shape[0]
+    rows, rank = c_buf.shape[1:]
+
+    def load(t):
+        req = peer(t % n, n) * req_local + t // n
+        slot = t % 2
+        return (pltpu.make_async_copy(c_hbm.at[req], c_buf.at[slot], c_sem.at[slot]),
+                pltpu.make_async_copy(k_hbm.at[req], k_buf.at[slot], k_sem.at[slot]))
+
+    def remote(t):
+        dst, m, slot = peer(t % n, n), t // n, t % depth
+        return pltpu.make_async_remote_copy(
+            src_ref=out_buf.at[slot], dst_ref=land_ref.at[m, me], send_sem=send_sem.at[slot],
+            recv_sem=recv_sem.at[m * n + me], device_id={"x": dst}, device_id_type=pl.DeviceIdType.MESH)
+
+    def own(t):
+        slot = t % depth
+        return pltpu.make_async_copy(out_buf.at[slot], land_ref.at[t // n, me], send_sem.at[slot])
+
+    def keep(t):
+        dst, m, slot = peer(t % n, n), t // n, t % depth
+        return pltpu.make_async_copy(out_buf.at[slot], rest_ref.at[dst, m - early], send_sem.at[slot])
+
+    def on_kind(t, act_remote, act_local):
+        is_tail = t >= early * n
+        is_own = t % n == n - 1
+
+        @pl.when(is_tail)
+        def _():
+            act_local(keep(t))
+
+        @pl.when(jnp.logical_and(jnp.logical_not(is_tail), is_own))
+        def _():
+            act_local(own(t))
+
+        @pl.when(jnp.logical_and(jnp.logical_not(is_tail), jnp.logical_not(is_own)))
+        def _():
+            act_remote(remote(t))
+
+    def start(t):
+        on_kind(t, lambda c: c.start(), lambda c: c.start())
+
+    def sent(t):
+        on_kind(t, lambda c: c.wait_send(), lambda c: c.wait())
+
+    barrier = pltpu.get_barrier_semaphore()
+    for j in range(n - 1):
+        pl.semaphore_signal(barrier, inc=1, device_id={"x": peer(j, n)}, device_id_type=pl.DeviceIdType.MESH)
+    for t in range(2):
+        for c in load(t):
+            c.start()
+    pl.semaphore_wait(barrier, n - 1)
+
+    @pl.loop(0, steps)
+    def _(t):
+        @pl.when(t >= depth)
+        def _():
+            sent(t - depth)
+
+        for c in load(t):
+            c.wait()
+        slot, out = t % 2, t % depth
+        left = lens_ref[peer(t % n, n) * req_local + t // n] - me * rows
+
+        @pl.loop(0, rows, step=STRIPE)
+        def _(r):
+            r = pl.multiple_of(r, STRIPE)
+            lat = c_buf[slot, pl.ds(r, STRIPE), :].astype(jnp.float32)
+            inv = lax.rsqrt(jnp.mean(lat * lat, axis=-1, keepdims=True) + NORM_EPS)
+            normed = lat * inv * gain_ref[...].astype(jnp.float32)
+            valid = r + lax.broadcasted_iota(jnp.int32, (STRIPE, 1), 0) < left
+            out_buf[out, pl.ds(r, STRIPE), :] = jnp.where(valid, normed, 0.0).astype(jnp.bfloat16)
+
+        key = k_buf[slot].astype(jnp.float32)
         half = key.shape[0] // 2
         lo, hi = key[:half], key[half:]
         cos, sin = cos_ref[...], sin_ref[...]
         valid = lax.broadcasted_iota(jnp.int32, (1, rows), 1) < left
-        store_rope(out_ref, 0, jnp.where(valid, lo * cos - hi * sin, 0.0).astype(jnp.bfloat16), rows, rank)
-        store_rope(out_ref, half, jnp.where(valid, hi * cos + lo * sin, 0.0).astype(jnp.bfloat16), rows, rank)
-
-
-def store_rope(out_ref, at, keys, rows, rank):
+        store_rope(out_buf, out, 0, jnp.where(valid, lo * cos - hi * sin, 0.0).astype(jnp.bfloat16), rows, rank)
+        store_rope(out_buf, out, half, jnp.where(valid, hi * cos + lo * sin, 0.0).astype(jnp.bfloat16), rows, rank)
+
+        @pl.when(t + 2 < steps)
+        def _():
+            for c in load(t + 2):
+                c.start()
+
+        @pl.when(t >= 1)
+        def _():
+            start(t - 1)
+
+    @pl.loop(steps - depth, steps - 1)
+    def _(t):
+        sent(t)
+
+    start(steps - 1)
+    sent(steps - 1)
+
+    @pl.loop(0, early)
+    def _(m):
+        @pl.loop(0, n - 1)
+        def _(j):
+            src = peer(j, n)
+            pltpu.make_async_remote_copy(
+                src_ref=land_ref.at[m, src], dst_ref=land_ref.at[m, src], send_sem=send_sem.at[0],
+                recv_sem=recv_sem.at[m * n + src], device_id={"x": src}, device_id_type=pl.DeviceIdType.MESH).wait_recv()
+
+
+def store_rope(out_ref, slot, at, keys, rows, rank):
     half = keys.shape[0]
     rest = rows - rank
     side = (at // half) * rest
-    out_ref[0, 0, rows + at : rows + at + half, :] = keys[:, :rank]
-    out_ref[0, 0, rows + 2 * half : rows + 3 * half, side : side + rest] = keys[:, rank:]
+    out_ref[slot, rows + at : rows + at + half, :] = keys[:, :rank]
+    out_ref[slot, rows + 2 * half : rows + 3 * half, side : side + rest] = keys[:, rank:]
 
 
 def load_rope(land_ref, kr_ref, rows, rank):
@@ -53,30 +152,32 @@
         kr_ref[0, at * half : (at + 1) * half, rank:] = land_ref[0, 0, rows + 2 * half : rows + 3 * half, at * rest : (at + 1) * rest]
 
 
-def pack(lens, c_raw, k_raw, gain, cos, sin, n, req_local, first, count):
+def send(lens, c_raw, k_raw, gain, cos, sin, n, req_local, tail):
     requests, rows, rank = c_raw.shape
     width = k_raw.shape[1]
     total = rows + rows * width // rank
-    req = lambda d, m, *_: (d * req_local + first + m, 0, 0)
-    fixed = lambda d, m, *_: (0, 0)
+    depth = DEPTH * n
+    hbm = pl.BlockSpec(memory_space=pl.ANY)
+    vmem = pl.BlockSpec(memory_space=pltpu.VMEM)
+    early = req_local - tail
     return pl.pallas_call(
-        functools.partial(pack_kernel, first, req_local),
-        grid_spec=pltpu.PrefetchScalarGridSpec(
-            num_scalar_prefetch=1,
-            grid=(n, count),
-            in_specs=[
-                pl.BlockSpec((1, rows, rank), req),
-                pl.BlockSpec((1, width, rows), req),
-                pl.BlockSpec((1, rank), fixed),
-                pl.BlockSpec((width // 2, rows), fixed),
-                pl.BlockSpec((width // 2, rows), fixed),
-            ],
-            out_specs=pl.BlockSpec((1, 1, total, rank), lambda d, m, *_: (d, m, 0, 0)),
-        ),
-        out_shape=jax.ShapeDtypeStruct((n, count, total, rank), jnp.bfloat16),
-        compiler_params=pltpu.CompilerParams(vmem_limit_bytes=VMEM_BYTES),
-        cost_estimate=pl.CostEstimate(flops=n * count * rows * rank * 100, bytes_accessed=n * count * total * rank * 4, transcendentals=0),
-        name=f"pack_{first}",
+        functools.partial(send_kernel, n, req_local, tail),
+        in_specs=[pl.BlockSpec(memory_space=pltpu.SMEM), hbm, hbm, vmem, vmem, vmem],
+        out_specs=[hbm, hbm],
+        out_shape=[jax.ShapeDtypeStruct((early, n, total, rank), jnp.bfloat16),
+                   jax.ShapeDtypeStruct((n, tail, total, rank), jnp.bfloat16)],
+        scratch_shapes=[
+            pltpu.VMEM((2, rows, rank), jnp.bfloat16),
+            pltpu.VMEM((2, width, rows), jnp.bfloat16),
+            pltpu.VMEM((depth, total, rank), jnp.bfloat16),
+            pltpu.SemaphoreType.DMA((2,)),
+            pltpu.SemaphoreType.DMA((2,)),
+            pltpu.SemaphoreType.DMA((depth,)),
+            pltpu.SemaphoreType.DMA((early * n,)),
+        ],
+        compiler_params=pltpu.CompilerParams(vmem_limit_bytes=VMEM_BYTES, collective_id=0, has_side_effects=True),
+        cost_estimate=pl.CostEstimate(flops=requests * rows * rank * 100, bytes_accessed=requests * total * rank * 4, transcendentals=0),
+        name="send",
     )(lens, c_raw, k_raw, gain, cos, sin)
 
 
@@ -121,7 +222,7 @@
         o_out[0] = (acc_scr[...] / l_scr[...]).astype(jnp.bfloat16)
 
 
-def attend(own_lens, landed, q_lat, q_rope, prev, n, rows, first, count):
+def attend(own_lens, landed, by_slot, q_lat, q_rope, prev, n, rows, first, count):
     req_local, heads, rank = q_lat.shape
     width = q_rope.shape[2]
     total = landed.shape[2]
@@ -131,7 +232,11 @@
         jax.ShapeDtypeStruct((req_local, width, n * rows), jnp.bfloat16),
         jax.ShapeDtypeStruct((req_local, heads, rank), jnp.bfloat16),
     ]
-    land = lambda m, i, lens: (jnp.minimum(i, (lens[m] - 1) // rows), m, 0, 0)
+
+    def land(m, i, lens):
+        i = jnp.minimum(i, (lens[m] - 1) // rows)
+        return (m, i, 0, 0) if by_slot else (i, m, 0, 0)
+
     slot = lambda m, i, lens: (first + m, 0, 0)
     any_spec = pl.BlockSpec(memory_space=pl.ANY)
     prev = list(prev) if prev is not None else []
@@ -175,14 +280,11 @@
         own_lens = lax.dynamic_slice_in_dim(seq_lens, lax.axis_index("x") * req_local, req_local)
         k_raw = jnp.swapaxes(k_raw, 1, 2)
         tables = (norm_gain[None, :], rope_cos.T, rope_sin.T)
-        landed, first = [], 0
-        for count in CHUNKS:
-            packed = pack(seq_lens, c_raw, k_raw, *tables, n, req_local, first, count)
-            landed.append((first, count, lax.all_to_all(packed, "x", 0, 0, tiled=True)))
-            first += count
-        outs = None
-        for first, count, block in landed:
-            outs = attend(own_lens, block, q_lat, q_rope, outs, n, rows, first, count)
+        early = req_local - TAIL
+        landed, rest = send(seq_lens, c_raw, k_raw, *tables, n, req_local, TAIL)
+        rest = lax.all_to_all(rest, "x", 0, 0, tiled=True)
+        outs = attend(own_lens, landed, True, q_lat, q_rope, None, n, rows, 0, early)
+        outs = attend(own_lens, rest, False, q_lat, q_rope, outs, n, rows, early, TAIL)
         return outs[0], jnp.swapaxes(outs[1], 1, 2), outs[2]
 
     return jax.shard_map(local_step, mesh=mesh, in_specs=(seq_spec, seq_spec, P(None), P("x", None), P("x", None), P("dp"), req_spec, req_spec), out_specs=(req_spec, req_spec, req_spec), check_vma=False)

time: 520 us -> 490 us (0.942)
  waiting for transfers between devices: 380 us -> 37.5 us
  Pallas kernels: 110 us -> 439 us
  starting transfers between devices: 21.4 us -> 5.16 us
    all_to_all x4 -> x1, waiting for transfers between devices: 380 us -> 37.5 us  [local_step(): rest = lax.all_to_all(rest, 'x', 0, 0, tiled=True)]
    pallas_call x4 -> x1, Pallas kernels: 57.5 us -> 390 us  [send(): pl.pallas_call(functools.partial(send_kernel, n, req_local, tail), in_spe...]
    all_to_all x4 -> x1, starting transfers between devices: 21.4 us -> 5.16 us  [local_step(): rest = lax.all_to_all(rest, 'x', 0, 0, tiled=True)]
    pallas_call x4 -> x2, Pallas kernels: 52.9 us -> 49 us  [attend(): pl.pallas_call(functools.partial(attend_kernel, n, scale), grid_spec=pltp...]
  transfers between devices with their start and end apart: 4 -> 1, of which waited for: 4 -> 1; matrix products, arithmetic and copies ran while one was open for 0% -> 0% of each run, Pallas kernels for 18% -> 9%
where the time goes in v2:
time: 490 us; the launch traced here: 485 us
  Pallas kernels  439 us (90%)
  waiting for transfers between devices  37.5 us (8%)
  starting transfers between devices  5.16 us (1%)
    pallas_call x1, Pallas kernels, send(): pl.pallas_call(functools.partial(send_kernel, n, req_local, tail), in_spe...  390 us
    pallas_call x2, Pallas kernels, attend(): pl.pallas_call(functools.partial(attend_kernel, n, scale), grid_spec=pltp...  49 us
    all_to_all x1, waiting for transfers between devices, local_step(): rest = lax.all_to_all(rest, 'x', 0, 0, tiled=True)  37.5 us
  transfers between devices with their start and end apart: 1, of which 1 were waited for; matrix products, arithmetic and copies ran while one was open for 0% of the time, Pallas kernels for 9%

profile of v2, /device:TPU:112, one launch (start us, length us, event | category | flops | bytes accessed | tf_op | source)
XLA Modules:
  0.0 485.0 jit_solution(7475787156978052685)
XLA Ops:
  0.6 1.3 broadcast_in_dim.3.gain_ref
  1.9 389.9 %send.1 = (bf16[5,8,864,512]{3,2,1,0:T(8,128)(2,1)}, bf16[8,1,864,512]{3,2,1,0:T(8,128)(2,1)}) custom-call(s32[48]{0:T(128)} %lens_ref.1, bf16[48,768,512]{2,1,0:T(8,128)(2,1)} %c_hbm.1, bf16[48,64,768]{2,1,0:T(8,128)(2,1)} %bitcast.5, bf16[1,512]{1,0:T(2,128)(2,1)} %broadcast_in_dim.3.gain_ref, f32[32,768]{1,0:T(8,128)} %bitcast.7, f32[32,768]{1,0:T(8,128)} %bitcast.8), custom_call_target="tpu_custom_call" | custom-call | flops 1887436800 | bytes 84934656 | tf_op jit(solution)/shard_map/send/pallas_call | solution.py:163
  391.8 0.0 copy-start.1
  391.8 0.0 copy-start
  391.8 5.2 %all-to-all-start = ((bf16[8,1,864,512]{3,2,1,0:T(8,128)(2,1)}), bf16[8,1,864,512]{3,2,1,0:T(8,128)(2,1)}, u32[]{:S(2)}, u32[]{:S(2)}) async-start(bf16[8,1,864,512]{3,2,1,0:T(8,128)(2,1)} %get-tuple-element.11), calls=%async_computation | async-start | bytes 14155776 | tf_op jit(solution)/shard_map/all_to_all | solution.py:285
  397.0 0.0 copy-done.1
  397.0 0.1 dynamic_slice.3
  397.1 0.0 copy-start.2
  397.1 0.6 slice.6.lens_ref
  397.7 0.0 copy-done
  397.7 0.8 copy.15.qr_ref
  398.5 0.0 copy-done.2
  398.5 41.3 %attend_0.1 = (bf16[6,6144,512]{2,1,0:T(8,128)(2,1)}, bf16[6,64,6144]{2,1,0:T(8,128)(2,1)}, bf16[6,128,512]{2,1,0:T(8,128)(2,1)}) custom-call(s32[5]{0:T(128)} %bitcast.9, bf16[5,8,864,512]{3,2,1,0:T(8,128)(2,1)} %get-tuple-element.12.land_ref, bf16[6,128,512]{2,1,0:T(8,128)(2,1)} %qa_ref.3, bf16[6,128,64]{2,1,0:T(8,128)(2,1)} %copy.15.qr_ref), custom_call_target="tpu_custom_call" | custom-call | flops 8556380160 | bytes 62914560 | tf_op jit(solution)/shard_map/attend_0/pallas_call | solution.py:243
  439.9 37.5 %all-to-all-done.land_ref = bf16[8,1,864,512]{3,2,1,0:T(8,128)(2,1)} async-done(((bf16[8,1,864,512]{3,2,1,0:T(8,128)(2,1)}), bf16[8,1,864,512]{3,2,1,0:T(8,128)(2,1)}, u32[]{:S(2)}, u32[]{:S(2)}) %all-to-all-start) | async-done | bytes 7077920 | tf_op jit(solution)/shard_map/all_to_all | solution.py:285
  477.3 7.7 %attend_5.1 = (bf16[6,6144,512]{2,1,0:T(8,128)(2,1)}, bf16[6,64,6144]{2,1,0:T(8,128)(2,1)}, bf16[6,128,512]{2,1,0:T(8,128)(2,1)}) custom-call(s32[1]{0:T(128)} %slice.6.lens_ref, bf16[8,1,864,512]{3,2,1,0:T(8,128)(2,1)} %all-to-all-done.land_ref, bf16[6,128,512]{2,1,0:T(8,128)(2,1)} %qa_ref.3, ...), custom_call_target="tpu_custom_call", output_to_operand_aliasing={{0}: (4, {}), {1}: (5, {}), {2}: (6, {})} | custom-call | flops 1711276032 | bytes 12582912 | tf_op jit(solution)/shard_map/attend_5/pallas_call | solution.py:243
Async XLA Ops:
  391.8 5.2 %copy-start.1 = (s32[48]{0:T(128)S(1)}, s32[48]{0:T(128)}, u32[]{:S(2)}) copy-start(s32[48]{0:T(128)} %lens_ref.1) | copy-start | bytes 580
  391.8 5.9 %copy-start = (bf16[6,128,64]{1,2,0:T(8,128)(2,1)S(1)}, bf16[6,128,64]{1,2,0:T(8,128)(2,1)}, u32[]{:S(2)}) copy-start(bf16[6,128,64]{1,2,0:T(8,128)(2,1)} %param.15) | copy-start | bytes 294916
  391.8 85.5 %all-to-all-start = ((bf16[8,1,864,512]{3,2,1,0:T(8,128)(2,1)}), bf16[8,1,864,512]{3,2,1,0:T(8,128)(2,1)}, u32[]{:S(2)}, u32[]{:S(2)}) async-start(bf16[8,1,864,512]{3,2,1,0:T(8,128)(2,1)} %get-tuple-element.11), calls=%async_computation | async-start | bytes 14155776 | tf_op jit(solution)/shard_map/all_to_all | solution.py:285
  397.1 1.4 copy-start.2

commit v3 on v0

v3 whole, which is shorter than its diff:
```python
import functools

import jax
import jax.numpy as jnp
from jax import lax
from jax.experimental import pallas as pl
from jax.experimental.pallas import tpu as pltpu
from jax.sharding import PartitionSpec as P

NORM_EPS = 1e-6
HALVES = 2
ROUNDS = 6
LOADS = 4
STRIPE = 128
LANES, SUBLANES = 128, 16
VMEM_BYTES = 60 * 1024 * 1024
ATTEND_BYTES = 52 * 1024 * 1024
MESH = pl.DeviceIdType.MESH
HBM = pl.BlockSpec(memory_space=pltpu.HBM)
VMEM = pl.BlockSpec(memory_space=pltpu.VMEM)
SMEM = pl.BlockSpec(memory_space=pltpu.SMEM)


def peer(j, n):
    me = lax.axis_index("x")
    chip, core = me // 2, me % 2
    far = j % 3
    last = j // (n - 2)
    hop = (1 - last) * (1 + 2 * far - 3 * (far // 2))
    other = (j // 3) % 2 * (1 - last) + last * (1 - j % (n - 2))
    return (chip + hop) % (n // 2) * 2 + (core + other) % 2


def rope_tiles(width, rows):
    for r in range(width // SUBLANES):
        for c in range(rows // LANES):
            yield (slice(r * SUBLANES, (r + 1) * SUBLANES), slice(c * LANES, (c + 1) * LANES),
                   slice(rows + c * SUBLANES, rows + (c + 1) * SUBLANES), slice(r * LANES, (r + 1) * LANES))


def send_kernel(n, req_local, lens_ref, c_hbm, k_hbm, gain_ref, cos_ref, sin_ref, land_ref, rest_ref,
                c_buf, k_buf, out_buf, c_sem, k_sem, send_sem, recv_sem):
    me = lax.axis_index("x")
    rounds = req_local * HALVES
    steps = rounds * n
    early = (rounds - 1) * n
    depth = out_buf.shape[0]
    rows, rank = c_buf.shape[1:]
    width = k_buf.shape[1]

    def load(t):
        req = peer(t % n, n) * req_local + t // n // HALVES
        first = pl.multiple_of(t // n % HALVES * rows, rows)
        slot = t % LOADS
        return (pltpu.make_async_copy(c_hbm.at[req, pl.ds(first, rows), :], c_buf.at[slot], c_sem.at[slot]),
                pltpu.make_async_copy(k_hbm.at[req, :, pl.ds(first, rows)], k_buf.at[slot], k_sem.at[slot]))

    def landing(t):
        return land_ref.at[t // n // HALVES, me, t // n % HALVES]

    def remote(t):
        slot = t % depth
        return pltpu.make_async_remote_copy(
            src_ref=out_buf.at[slot], dst_ref=landing(t), send_sem=send_sem.at[slot],
            recv_sem=recv_sem.at[t // n * n + me], device_id={"x": peer(t % n, n)}, device_id_type=MESH)

    def own(t):
        return pltpu.make_async_copy(out_buf.at[t % depth], landing(t), send_sem.at[t % depth])

    def keep(t):
        return pltpu.make_async_copy(out_buf.at[t % depth], rest_ref.at[peer(t % n, n)], send_sem.at[t % depth])

    def on_kind(t, act_remote, act_local):
        is_own = t % n == n - 1

        @pl.when(t >= early)
        def _():
            act_local(keep(t))

        @pl.when(jnp.logical_and(t < early, is_own))
        def _():
            act_local(own(t))

        @pl.when(jnp.logical_and(t < early, jnp.logical_not(is_own)))
        def _():
            act_remote(remote(t))

    def start(t):
        on_kind(t, lambda c: c.start(), lambda c: c.start())

    def sent(t):
        on_kind(t, lambda c: c.wait_send(), lambda c: c.wait())

    def pack(t):
        for c in load(t):
            c.wait()
        slot, out = t % LOADS, t % depth
        first = t // n % HALVES * rows
        left = lens_ref[peer(t % n, n) * req_local + t // n // HALVES] - me * (rows * HALVES) - first
        gain = gain_ref[...].astype(jnp.float32)

        @pl.loop(0, rows, step=STRIPE)
        def _(r):
            r = pl.multiple_of(r, STRIPE)
            lat = c_buf[slot, pl.ds(r, STRIPE), :].astype(jnp.float32)
            inv = lax.rsqrt(jnp.mean(lat * lat, axis=-1, keepdims=True) + NORM_EPS)
            valid = r + lax.broadcasted_iota(jnp.int32, (STRIPE, 1), 0) < left
            out_buf[out, pl.ds(r, STRIPE), :] = jnp.where(valid, lat * inv * gain, 0.0).astype(jnp.bfloat16)

        key = k_buf[slot].astype(jnp.float32)
        half = width // 2
        lo, hi = key[:half], key[half:]
        first = pl.multiple_of(first, LANES)
        cos, sin = cos_ref[:, pl.ds(first, rows)], sin_ref[:, pl.ds(first, rows)]
        valid = lax.broadcasted_iota(jnp.int32, (1, rows), 1) < left
        rotated = (jnp.where(valid, lo * cos - hi * sin, 0.0).astype(jnp.bfloat16),
                   jnp.where(valid, hi * cos + lo * sin, 0.0).astype(jnp.bfloat16))
        for kr_rows, kr_cols, to_rows, to_cols in rope_tiles(width, rows):
            part, at = kr_rows.start // half, kr_rows.start % half
            out_buf[out, to_rows, to_cols] = rotated[part][at : at + SUBLANES, kr_cols]

    barrier = pltpu.get_barrier_semaphore()
    for j in range(n - 1):
        pl.semaphore_signal(barrier, inc=1, device_id={"x": peer(j, n)}, device_id_type=MESH)
    for t in range(LOADS):
        for c in load(t):
            c.start()
    pack(0)
    for c in load(LOADS):
        c.start()
    pl.semaphore_wait(barrier, n - 1)

    @pl.loop(1, steps)
    def _(t):
        @pl.when(t >= depth)
        def _():
            sent(t - depth)

        pack(t)

        @pl.when(t + LOADS < steps)
        def _():
            for c in load(t + LOADS):
                c.start()

        start(t - 1)

    @pl.loop(steps - depth, steps - 1)
    def _(t):
        sent(t)

    start(steps - 1)
    sent(steps - 1)

    @pl.loop(0, rounds - 1)
    def _(r):
        @pl.loop(0, n - 1)
        def _(j):
            src = peer(j, n)
            piece = land_ref.at[r // HALVES, src, r % HALVES]
            pltpu.make_async_remote_copy(
                src_ref=piece, dst_ref=piece, send_sem=send_sem.at[0], recv_sem=recv_sem.at[r * n + src],
                device_id={"x": src}, device_id_type=MESH).wait_recv()


def send(lens, c_raw, k_raw, gain, cos, sin, n, req_local):
    requests, block, rank = c_raw.shape
    width = k_raw.shape[1]
    rows = block // HALVES
    total = rows + rows * width // rank
    depth = ROUNDS * n
    return pl.pallas_call(
        functools.partial(send_kernel, n, req_local),
        in_specs=[SMEM, HBM, HBM, VMEM, VMEM, VMEM],
        out_specs=[HBM, HBM],
        out_shape=[jax.ShapeDtypeStruct((req_local, n, HALVES, total, rank), jnp.bfloat16),
                   jax.ShapeDtypeStruct((n, total, rank), jnp.bfloat16)],
        scratch_shapes=[
            pltpu.VMEM((LOADS, rows, rank), jnp.bfloat16),
            pltpu.VMEM((LOADS, width, rows), jnp.bfloat16),
            pltpu.VMEM((depth, total, rank), jnp.bfloat16),
            pltpu.SemaphoreType.DMA((LOADS,)),
            pltpu.SemaphoreType.DMA((LOADS,)),
            pltpu.SemaphoreType.DMA((depth,)),
            pltpu.SemaphoreType.DMA(((req_local * HALVES - 1) * n,)),
        ],
        compiler_params=pltpu.CompilerParams(vmem_limit_bytes=VMEM_BYTES, collective_id=0, has_side_effects=True),
        cost_estimate=pl.CostEstimate(flops=requests * block * rank * 100, bytes_accessed=requests * block * rank * 4, transcendentals=0),
        name="send",
    )(lens, c_raw, k_raw, gain, cos, sin)


def stream(n, req_local, scale, group, length, land, queries, c_out, kr_out, state, buf, kr_buf, zero_c, zero_k, in_sem, c_sem, k_sem, ahead):
    first_req, count, first_piece, pieces = group
    m_ref, l_ref, acc_ref = state
    depth = buf.shape[0]
    rank = buf.shape[3]
    width = kr_buf.shape[1]
    rows = buf.shape[2] * rank // (rank + width)
    span = rows * HALVES
    steps = count * n

    def used(t):
        return t % n * span + first_piece * rows < length(first_req + t // n)

    def load(t):
        return pltpu.make_async_copy(land(t // n, t % n), buf.at[t % depth, pl.ds(0, pieces)], in_sem.at[t % depth])

    def stores(t):
        slot, req = t % depth, first_req + t // n
        at = pl.multiple_of(t % n * span + first_piece * rows, rows)
        kr = pltpu.make_async_copy(kr_buf.at[slot, :, pl.ds(0, pieces * rows)], kr_out.at[req, :, pl.ds(at, pieces * rows)], k_sem.at[slot])
        cs = [pltpu.make_async_copy(buf.at[slot, h, pl.ds(0, rows), :], c_out.at[req, pl.ds(at + h * rows, rows), :], c_sem.at[slot, h]) for h in range(pieces)]
        return cs + [kr]

    def blanks(t):
        slot, req = t % depth, first_req + t // n
        at = pl.multiple_of(t % n * span + first_piece * rows, rows)
        kr = pltpu.make_async_copy(zero_k.at[:, pl.ds(0, pieces * rows)], kr_out.at[req, :, pl.ds(at, pieces * rows)], k_sem.at[slot])
        cs = [pltpu.make_async_copy(zero_c, c_out.at[req, pl.ds(at + h * rows, rows), :], c_sem.at[slot, h]) for h in range(pieces)]
        return cs + [kr]

    def fetch(t):
        @pl.when(used(t))
        def _():
            load(t).start()

    def work(t):
        slot, req = t % depth, first_req + t // n
        load(t).wait()
        for h in range(pieces):
            for kr_rows, kr_cols, from_rows, from_cols in rope_tiles(width, rows):
                cols = slice(h * rows + kr_cols.start, h * rows + kr_cols.stop)
                kr_buf[slot, kr_rows, cols] = buf[slot, h, from_rows, from_cols]
        for c in stores(t):
            c.start()
        qa, qr = queries(t)
        scores = []
        for h in range(pieces):
            s = lax.dot_general(qa, buf[slot, h, :rows, :], (((1,), (1,)), ((), ())), preferred_element_type=jnp.float32)
            s = s + lax.dot_general(qr, kr_buf[slot, :, h * rows : (h + 1) * rows], (((0,), (0,)), ((), ())), preferred_element_type=jnp.float32)
            pos = t % n * span + (first_piece + h) * rows + lax.broadcasted_iota(jnp.int32, (1, rows), 1)
            scores.append(jnp.where(pos < length(req), s * scale, -1e30))
        m_old = m_ref[...]
        m_new = m_old
        for s in scores:
            m_new = jnp.maximum(m_new, jnp.max(s, axis=-1, keepdims=True))
        alpha = jnp.exp(m_old - m_new)
        total, acc = l_ref[...] * alpha, acc_ref[...] * alpha
        for h, s in enumerate(scores):
            p = jnp.exp(s - m_new)
            total = total + jnp.sum(p, axis=-1, keepdims=True)
            acc = acc + jnp.dot(p.astype(jnp.bfloat16), buf[slot, h, :rows, :], preferred_element_type=jnp.float32)
        m_ref[...], l_ref[...], acc_ref[...] = m_new, total, acc

    def body(t, begin, finish):
        @pl.when(t % n == 0)
        def _():
            begin()

        @pl.when(used(t))
        def _():
            work(t)

        @pl.when(jnp.logical_not(used(t)))
        def _():
            for c in blanks(t):
                c.start()

        @pl.when(t + ahead < steps)
        def _():
            @pl.when(t + ahead >= depth)
            def _():
                for c in stores(t + ahead - depth):
                    c.wait()

            fetch(t + ahead)

        @pl.when(t % n == n - 1)
        def _():
            finish(first_req + t // n)

    def run(begin, finish):
        for t in range(min(ahead, steps)):
            fetch(t)

        @pl.loop(0, steps)
        def _(t):
            body(t, begin, finish)

        @pl.loop(max(steps - depth, 0), steps)
        def _(t):
            for c in stores(t):
                c.wait()

    return run


def clear(state):
    m_ref, l_ref, acc_ref = state
    m_ref[...] = jnp.full_like(m_ref, -1e30)
    l_ref[...] = jnp.zeros_like(l_ref)
    acc_ref[...] = jnp.zeros_like(acc_ref)


def first_kernel(n, req_local, scale, lens_ref, land_ref, qa_ref, qr_ref, c_out, kr_out, o_out, part_out,
                 m_ref, l_ref, acc_ref, part_ref, part_sem, zero_c, zero_k, buf, in_sem, kr_buf, c_sem, k_sem):
    length = lambda m: lens_ref[lax.axis_index("x") * req_local + m]
    zero_c[...] = jnp.zeros_like(zero_c)
    zero_k[...] = jnp.zeros_like(zero_k)
    state = (m_ref, l_ref, acc_ref)
    rest = (c_out, kr_out, state, buf, kr_buf, zero_c, zero_k, in_sem, c_sem, k_sem, buf.shape[0] // 2)
    last = req_local - 1
    rank = acc_ref.shape[1]

    def finish(m):
        o_out[m] = (acc_ref[...] / l_ref[...]).astype(jnp.bfloat16)

    def hand_over(m):
        part_ref[:, :rank] = acc_ref[...]
        part_ref[:, rank : rank + LANES] = jnp.broadcast_to(m_ref[...], (part_ref.shape[0], LANES))
        part_ref[:, rank + LANES :] = jnp.broadcast_to(l_ref[...], (part_ref.shape[0], LANES))
        copy = pltpu.make_async_copy(part_ref, part_out, part_sem)
        copy.start()
        copy.wait()

    whole = lambda m, i: land_ref.at[m, i]
    stream(n, req_local, scale, (0, last, 0, HALVES), length, whole, lambda t: (qa_ref[t // n], qr_ref[t // n]), *rest)(lambda: clear(state), finish)
    piece = lambda m, i: land_ref.at[last, i, pl.ds(0, HALVES - 1)]
    stream(n, req_local, scale, (last, 1, 0, HALVES - 1), length, piece, lambda t: (qa_ref[last], qr_ref[last]), *rest)(lambda: clear(state), hand_over)


def last_kernel(n, req_local, scale, lens_ref, land_ref, qa_hbm, qr_hbm, part_hbm, c_old, kr_old, o_old, c_out, kr_out, o_out,
                m_ref, l_ref, acc_ref, qa_ref, qr_ref, part_ref, o_buf, sems, zero_c, zero_k, buf, in_sem, kr_buf, c_sem, k_sem):
    length = lambda m: lens_ref[lax.axis_index("x") * req_local + m]
    last = req_local - 1
    state = (m_ref, l_ref, acc_ref)
    rank = acc_ref.shape[1]
    copies = [pltpu.make_async_copy(qa_hbm.at[last], qa_ref, sems.at[0]), pltpu.make_async_copy(qr_hbm.at[last], qr_ref, sems.at[1]),
              pltpu.make_async_copy(part_hbm, part_ref, sems.at[2])]
    for c in copies:
        c.start()
    zero_c[...] = jnp.zeros_like(zero_c)
    zero_k[...] = jnp.zeros_like(zero_k)

    def begin():
        clear(state)
        for c in copies:
            c.wait()

    def finish(m):
        m_part, l_part, acc_part = part_ref[:, rank : rank + 1], part_ref[:, rank + LANES : rank + LANES + 1], part_ref[:, :rank]
        m_new = jnp.maximum(m_ref[...], m_part)
        here, there = jnp.exp(m_ref[...] - m_new), jnp.exp(m_part - m_new)
        total = l_ref[...] * here + l_part * there
        o_buf[...] = ((acc_ref[...] * here + acc_part * there) / total).astype(jnp.bfloat16)
        copy = pltpu.make_async_copy(o_buf, o_out.at[m], sems.at[3])
        copy.start()
        copy.wait()

    stream(n, req_local, scale, (last, 1, HALVES - 1, 1), length, lambda m, i: land_ref.at[i], lambda t: (qa_ref[...], qr_ref[...]), c_out, kr_out, state, buf, kr_buf,
           zero_c, zero_k, in_sem, c_sem, k_sem, buf.shape[0])(begin, finish)


def attend(lens, landed, rest, q_lat, q_rope, n, block):
    req_local, heads, rank = q_lat.shape
    width = q_rope.shape[1]
    rows = block // HALVES
    total = rest.shape[2]
    scale = (rank + width) ** -0.5
    caches = [jax.ShapeDtypeStruct((req_local, n * block, rank), jnp.bfloat16),
              jax.ShapeDtypeStruct((req_local, width, n * block), jnp.bfloat16),
              jax.ShapeDtypeStruct((req_local, heads, rank), jnp.bfloat16)]
    part = jax.ShapeDtypeStruct((heads, rank + 2 * LANES), jnp.float32)
    state = [pltpu.VMEM((heads, 1), jnp.float32), pltpu.VMEM((heads, 1), jnp.float32), pltpu.VMEM((heads, rank), jnp.float32)]

    def scratch(depth, pieces):
        return [pltpu.VMEM((rows, rank), jnp.bfloat16), pltpu.VMEM((width, pieces * rows), jnp.bfloat16)], [
            pltpu.VMEM((depth, width, pieces * rows), jnp.bfloat16), pltpu.SemaphoreType.DMA((depth, pieces)), pltpu.SemaphoreType.DMA((depth,))]

    params = pltpu.CompilerParams(vmem_limit_bytes=ATTEND_BYTES)
    flops = req_local * n * block * heads * (2 * rank + width) * 2
    zeros, stores = scratch(n, HALVES)
    *outs, first_part = pl.pallas_call(
        functools.partial(first_kernel, n, req_local, scale),
        in_specs=[SMEM, HBM, VMEM, VMEM],
        out_specs=[HBM, HBM, VMEM, HBM],
        out_shape=caches + [part],
        scratch_shapes=state + [pltpu.VMEM(part.shape, part.dtype), pltpu.SemaphoreType.DMA] + zeros + [
            pltpu.VMEM((n, HALVES, total, rank), jnp.bfloat16), pltpu.SemaphoreType.DMA((n,))] + stores,
        compiler_params=params,
        cost_estimate=pl.CostEstimate(flops=flops, bytes_accessed=req_local * n * block * rank * 4, transcendentals=0),
        name="attend_first",
    )(lens, landed, q_lat, q_rope)
    zeros, stores = scratch(n, 1)
    return pl.pallas_call(
        functools.partial(last_kernel, n, req_local, scale),
        in_specs=[SMEM] + [HBM] * 7,
        out_specs=[HBM] * 3,
        out_shape=caches,
        scratch_shapes=state + [pltpu.VMEM((heads, rank), jnp.bfloat16), pltpu.VMEM((width, heads), jnp.bfloat16), pltpu.VMEM(part.shape, part.dtype),
                                pltpu.VMEM((heads, rank), jnp.bfloat16), pltpu.SemaphoreType.DMA((4,))] + zeros + [
            pltpu.VMEM((n, 1, total, rank), jnp.bfloat16), pltpu.SemaphoreType.DMA((n,))] + stores,
        input_output_aliases={5: 0, 6: 1, 7: 2},
        compiler_params=params,
        cost_estimate=pl.CostEstimate(flops=flops // req_local // HALVES, bytes_accessed=n * block * rank * 2, transcendentals=0),
        name="attend_last",
    )(lens, rest, q_lat, q_rope, first_part, *outs)


def solution(mesh):
    seq_spec = P("dp", "x", None)
    req_spec = P(("dp", "x"), None, None)
    n = mesh.shape["x"]

    def local_step(c_raw, k_raw, norm_gain, rope_cos, rope_sin, seq_lens, q_lat, q_rope):
        landed, rest = send(seq_lens, c_raw, jnp.swapaxes(k_raw, 1, 2), norm_gain, rope_cos.T, rope_sin.T, n, q_lat.shape[0])
        rest = lax.all_to_all(rest, "x", 0, 0, tiled=True)[:, None]
        c_cache, kr_cache, o_lat = attend(seq_lens, landed, rest, q_lat, jnp.swapaxes(q_rope, 1, 2), n, c_raw.shape[1])
        return c_cache, jnp.swapaxes(kr_cache, 1, 2), o_lat

    return jax.shard_map(local_step, mesh=mesh, in_specs=(seq_spec, seq_spec, P(None), P("x", None), P("x", None), P("dp"), req_spec, req_spec), out_specs=(req_spec, req_spec, req_spec), check_vma=False)
```

time: 581 us -> 495 us (0.85)
  the two profiles are of different devices: /device:TPU:112 before, /device:TPU:120 now
where the time goes in v3:
time: 495 us; the launch traced here: 485 us
  Pallas kernels  480 us (97%)
    pallas_call x1, Pallas kernels, send(): pl.pallas_call(functools.partial(send_kernel, n, req_local), in_specs=[SM...  428 us
    pallas_call x1, Pallas kernels, attend(): pl.pallas_call(functools.partial(first_kernel, n, req_local, scale), in_s...  46.6 us
  transfers between devices with their start and end apart: 1, of which 0 were waited for; matrix products, arithmetic and copies ran while one was open for 0% of the time, Pallas kernels for 10%

profile of v3, /device:TPU:120, one launch (start us, length us, event | category | flops | bytes accessed | tf_op | source)
XLA Modules:
  0.0 485.3 jit_solution(11946796340170146740)
XLA Ops:
  0.6 427.8 %send.1 = (bf16[6,8,2,432,512]{4,3,2,1,0:T(8,128)(2,1)}, bf16[8,432,512]{2,1,0:T(8,128)(2,1)}) custom-call(s32[48]{0:T(128)} %lens_ref.5, bf16[48,768,512]{2,1,0:T(8,128)(2,1)} %c_hbm.1, bf16[48,64,768]{2,1,0:T(8,128)(2,1)} %bitcast.8, bf16[512]{0:T(512)(128)(2,1)} %gain_ref.1, f32[32,768]{1,0:T(8,128)} %bitcast.10, f32[32,768]{1,0:T(8,128)} %bitcast.11), custom_call_target="tpu_custom_call" | custom-call | flops 1887436800 | bytes 75497472 | tf_op jit(solution)/shard_map/send/pallas_call | solution.py:172
  428.5 0.0 copy-start
  428.5 0.0 copy-start.1
  428.5 0.0 copy-start.2
  428.5 4.8 all-to-all-start
  433.3 0.0 copy-done
  433.4 0.0 copy-done.1
  433.4 0.0 copy-done.2
  433.4 46.6 %attend_first.1 = (bf16[6,6144,512]{2,1,0:T(8,128)(2,1)}, bf16[6,64,6144]{2,1,0:T(8,128)(2,1)}, bf16[6,128,512]{2,1,0:T(8,128)(2,1)}, f32[128,768]{1,0:T(8,128)S(1)}) custom-call(s32[48]{0:T(128)S(1)} %copy-done.2, bf16[6,8,2,432,512]{4,3,2,1,0:T(8,128)(2,1)} %get-tuple-element.13.land_ref, bf16[6,128,512]{2,1,0:T(8,128)(2,1)S(1)} %copy-done, ...), custom_call_target="tpu_custom_call" | custom-call | flops 10267656192 | bytes 75497472 | tf_op jit(solution)/shard_map/attend_first/pallas_call | solution.py:384
  480.0 0.0 all-to-all-done
  480.0 5.3 %attend_last.1 = (bf16[6,6144,512]{2,1,0:T(8,128)(2,1)}, bf16[6,64,6144]{2,1,0:T(8,128)(2,1)}, bf16[6,128,512]{2,1,0:T(8,128)(2,1)}) custom-call(s32[48]{0:T(128)S(1)} %copy-done.2, bf16[8,1,432,512]{3,2,1,0:T(8,128)(2,1)} %bitcast.3.land_ref, bf16[6,128,512]{2,1,0:T(8,128)(2,1)S(1)} %copy-done, ...), custom_call_target="tpu_custom_call", output_to_operand_aliasing={{0}: (5, {}), {1}: (6, {}), {2}: (7, {})} | custom-call | flops 855638016 | bytes 6291456 | tf_op jit(solution)/shard_map/attend_last/pallas_call | solution.py:396
Async XLA Ops:
  428.5 4.9 %copy-start = (bf16[6,128,512]{2,1,0:T(8,128)(2,1)S(1)}, bf16[6,128,512]{2,1,0:T(8,128)(2,1)}, u32[]{:S(2)}) copy-start(bf16[6,128,512]{2,1,0:T(8,128)(2,1)} %qa_hbm.1) | copy-start | bytes 2359300
  428.5 4.9 %copy-start.1 = (bf16[6,128,64]{1,2,0:T(8,128)(2,1)S(1)}, bf16[6,128,64]{1,2,0:T(8,128)(2,1)}, u32[]{:S(2)}) copy-start(bf16[6,128,64]{1,2,0:T(8,128)(2,1)} %param.15) | copy-start | bytes 294916
  428.5 4.9 %copy-start.2 = (s32[48]{0:T(128)S(1)}, s32[48]{0:T(128)}, u32[]{:S(2)}) copy-start(s32[48]{0:T(128)} %lens_ref.5) | copy-start | bytes 580
  428.5 51.5 %all-to-all-start = ((bf16[8,432,512]{2,1,0:T(8,128)(2,1)}), bf16[8,432,512]{2,1,0:T(8,128)(2,1)}, u32[]{:S(2)}, u32[]{:S(2)}) async-start(bf16[8,432,512]{2,1,0:T(8,128)(2,1)} %get-tuple-element.12), calls=%async_computation | async-start | bytes 7077888 | tf_op jit(solution)/shard_map/all_to_all | solution.py:418

commit v4 on v3

--- a/solution.py
+++ b/solution.py
@@ -8,9 +8,11 @@
 from jax.sharding import PartitionSpec as P
 
 NORM_EPS = 1e-6
-HALVES = 2
+PIECES = 3
 ROUNDS = 6
 LOADS = 4
+RING = 12
+AHEAD = 3
 STRIPE = 128
 LANES, SUBLANES = 128, 16
 VMEM_BYTES = 60 * 1024 * 1024
@@ -38,10 +40,39 @@
                    slice(rows + c * SUBLANES, rows + (c + 1) * SUBLANES), slice(r * LANES, (r + 1) * LANES))
 
 
-def send_kernel(n, req_local, lens_ref, c_hbm, k_hbm, gain_ref, cos_ref, sin_ref, land_ref, rest_ref,
-                c_buf, k_buf, out_buf, c_sem, k_sem, send_sem, recv_sem):
+def clear(state):
+    m_ref, l_ref, acc_ref = state
+    m_ref[...] = jnp.full_like(m_ref, -1e30)
+    l_ref[...] = jnp.zeros_like(l_ref)
+    acc_ref[...] = jnp.zeros_like(acc_ref)
+
+
+def fold(state, qa, qr, pieces, first, length, scale):
+    m_ref, l_ref, acc_ref = state
+    scores = []
+    for h, (lat, kr) in enumerate(pieces):
+        s = lax.dot_general(qa, lat, (((1,), (1,)), ((), ())), preferred_element_type=jnp.float32)
+        s = s + lax.dot_general(qr, kr, (((0,), (0,)), ((), ())), preferred_element_type=jnp.float32)
+        rows = lat.shape[0]
+        pos = first + h * rows + lax.broadcasted_iota(jnp.int32, (1, rows), 1)
+        scores.append(jnp.where(pos < length, s * scale, -1e30))
+    m_old = m_ref[...]
+    m_new = m_old
+    for s in scores:
+        m_new = jnp.maximum(m_new, jnp.max(s, axis=-1, keepdims=True))
+    alpha = jnp.exp(m_old - m_new)
+    total, acc = l_ref[...] * alpha, acc_ref[...] * alpha
+    for s, (lat, _) in zip(scores, pieces):
+        p = jnp.exp(s - m_new)
+        total = total + jnp.sum(p, axis=-1, keepdims=True)
+        acc = acc + jnp.dot(p.astype(jnp.bfloat16), lat, preferred_element_type=jnp.float32)
+    m_ref[...], l_ref[...], acc_ref[...] = m_new, total, acc
+
+
+def send_kernel(n, req_local, scale, lens_ref, c_hbm, k_hbm, gain_ref, cos_ref, sin_ref, qa_ref, qr_ref, land_ref, rest_ref, o_out,
+                c_buf, k_buf, out_buf, c_sem, k_sem, send_sem, recv_sem, m_ref, l_ref, acc_ref, fold_buf, kr_buf, fold_sem):
     me = lax.axis_index("x")
-    rounds = req_local * HALVES
+    rounds = req_local * PIECES
     steps = rounds * n
     early = (rounds - 1) * n
     depth = out_buf.shape[0]
@@ -49,14 +80,14 @@
     width = k_buf.shape[1]
 
     def load(t):
-        req = peer(t % n, n) * req_local + t // n // HALVES
-        first = pl.multiple_of(t // n % HALVES * rows, rows)
+        req = peer(t % n, n) * req_local + t // n // PIECES
+        first = pl.multiple_of(t // n % PIECES * rows, rows)
         slot = t % LOADS
         return (pltpu.make_async_copy(c_hbm.at[req, pl.ds(first, rows), :], c_buf.at[slot], c_sem.at[slot]),
                 pltpu.make_async_copy(k_hbm.at[req, :, pl.ds(first, rows)], k_buf.at[slot], k_sem.at[slot]))
 
     def landing(t):
-        return land_ref.at[t // n // HALVES, me, t // n % HALVES]
+        return land_ref.at[t // n // PIECES, me, t // n % PIECES]
 
     def remote(t):
         slot = t % depth
@@ -95,8 +126,8 @@
         for c in load(t):
             c.wait()
         slot, out = t % LOADS, t % depth
-        first = t // n % HALVES * rows
-        left = lens_ref[peer(t % n, n) * req_local + t // n // HALVES] - me * (rows * HALVES) - first
+        first = t // n % PIECES * rows
+        left = lens_ref[peer(t % n, n) * req_local + t // n // PIECES] - me * (rows * PIECES) - first
         gain = gain_ref[...].astype(jnp.float32)
 
         @pl.loop(0, rows, step=STRIPE)
@@ -130,51 +161,95 @@
         c.start()
     pl.semaphore_wait(barrier, n - 1)
 
-    @pl.loop(1, steps)
+    state = (m_ref, l_ref, acc_ref)
+    per_req = PIECES * n
+    folds = (req_local - 1) * per_req
+    lag = depth + n
+
+    def received(a):
+        src = peer(a % n, n)
+        piece = land_ref.at[a // per_req, src, a // n % PIECES]
+        pltpu.make_async_remote_copy(
+            src_ref=piece, dst_ref=piece, send_sem=send_sem.at[0], recv_sem=recv_sem.at[a // n * n + src],
+            device_id={"x": src}, device_id_type=MESH).wait_recv()
+
+    def fetch(a):
+        return pltpu.make_async_copy(land_ref.at[a // per_req, peer(a % n, n), a // n % PIECES], fold_buf.at[a % (AHEAD + 1)], fold_sem.at[a % (AHEAD + 1)])
+
+    @pl.loop(1, folds + lag)
     def _(t):
         @pl.when(t >= depth)
         def _():
             sent(t - depth)
 
-        pack(t)
-
-        @pl.when(t + LOADS < steps)
-        def _():
-            for c in load(t + LOADS):
-                c.start()
-
-        start(t - 1)
-
-    @pl.loop(steps - depth, steps - 1)
+        @pl.when(t < steps)
+        def _():
+            pack(t)
+
+            @pl.when(t + LOADS < steps)
+            def _():
+                for c in load(t + LOADS):
+                    c.start()
+
+        @pl.when(t <= steps)
+        def _():
+            start(t - 1)
+
+        arriving = t - lag + AHEAD
+
+        @pl.when(jnp.logical_and(arriving >= 0, arriving < folds))
+        def _():
+            @pl.when(arriving % n < n - 1)
+            def _():
+                received(arriving)
+
+            fetch(arriving).start()
+
+        a = t - lag
+
+        @pl.when(a >= 0)
+        def _():
+            m, src, slot = a // per_req, peer(a % n, n), a % (AHEAD + 1)
+
+            @pl.when(a % per_req == 0)
+            def _():
+                clear(state)
+
+            fetch(a).wait()
+            for kr_rows, kr_cols, from_rows, from_cols in rope_tiles(width, rows):
+                kr_buf[kr_rows, kr_cols] = fold_buf[slot, from_rows, from_cols]
+            first = (src * PIECES + a // n % PIECES) * rows
+            fold(state, qa_ref[m], qr_ref[m], [(fold_buf[slot, :rows, :], kr_buf[...])], first, lens_ref[me * req_local + m], scale)
+
+            @pl.when(a % per_req == per_req - 1)
+            def _():
+                o_out[m] = (acc_ref[...] / l_ref[...]).astype(jnp.bfloat16)
+
+    @pl.loop(folds + lag - depth, steps)
     def _(t):
         sent(t)
 
-    start(steps - 1)
-    sent(steps - 1)
-
-    @pl.loop(0, rounds - 1)
-    def _(r):
-        @pl.loop(0, n - 1)
-        def _(j):
-            src = peer(j, n)
-            piece = land_ref.at[r // HALVES, src, r % HALVES]
-            pltpu.make_async_remote_copy(
-                src_ref=piece, dst_ref=piece, send_sem=send_sem.at[0], recv_sem=recv_sem.at[r * n + src],
-                device_id={"x": src}, device_id_type=MESH).wait_recv()
-
-
-def send(lens, c_raw, k_raw, gain, cos, sin, n, req_local):
+    @pl.loop(folds, early)
+    def _(a):
+        @pl.when(a % n < n - 1)
+        def _():
+            received(a)
+
+
+def send(lens, c_raw, k_raw, gain, cos, sin, q_lat, q_rope, n):
+    req_local, heads, _ = q_lat.shape
     requests, block, rank = c_raw.shape
     width = k_raw.shape[1]
-    rows = block // HALVES
+    rows = block // PIECES
     total = rows + rows * width // rank
     depth = ROUNDS * n
     return pl.pallas_call(
-        functools.partial(send_kernel, n, req_local),
-        in_specs=[SMEM, HBM, HBM, VMEM, VMEM, VMEM],
-        out_specs=[HBM, HBM],
-        out_shape=[jax.ShapeDtypeStruct((req_local, n, HALVES, total, rank), jnp.bfloat16),
-                   jax.ShapeDtypeStruct((n, total, rank), jnp.bfloat16)],
+        functools.partial(send_kernel, n, req_local, (rank + width) ** -0.5),
+        in_specs=[SMEM, HBM, HBM] + [VMEM] * 5,
+        out_specs=[HBM, HBM, VMEM],
+        out_shape=[jax.ShapeDtypeStruct((req_local, n, PIECES, total, rank), jnp.bfloat16),
+                   jax.ShapeDtypeStruct((n, total, rank), jnp.bfloat16),
+                   jax.ShapeDtypeStruct((req_local - 1, heads, rank), jnp.bfloat16)],
         scratch_shapes=[
             pltpu.VMEM((LOADS, rows, rank), jnp.bfloat16),
             pltpu.VMEM((LOADS, width, rows), jnp.bfloat16),
@@ -182,22 +257,27 @@
             pltpu.SemaphoreType.DMA((LOADS,)),
             pltpu.SemaphoreType.DMA((LOADS,)),
             pltpu.SemaphoreType.DMA((depth,)),
-            pltpu.SemaphoreType.DMA(((req_local * HALVES - 1) * n,)),
+            pltpu.SemaphoreType.DMA(((req_local * PIECES - 1) * n,)),
+            pltpu.VMEM((heads, 1), jnp.float32),
+            pltpu.VMEM((heads, 1), jnp.float32),
+            pltpu.VMEM((heads, rank), jnp.float32),
+            pltpu.VMEM((AHEAD + 1, total, rank), jnp.bfloat16),
+            pltpu.VMEM((width, rows), jnp.bfloat16),
+            pltpu.SemaphoreType.DMA((AHEAD + 1,)),
         ],
         compiler_params=pltpu.CompilerParams(vmem_limit_bytes=VMEM_BYTES, collective_id=0, has_side_effects=True),
         cost_estimate=pl.CostEstimate(flops=requests * block * rank * 100, bytes_accessed=requests * block * rank * 4, transcendentals=0),
         name="send",
-    )(lens, c_raw, k_raw, gain, cos, sin)
+    )(lens, c_raw, k_raw, gain, cos, sin, q_lat, q_rope)
 
 
 def stream(n, req_local, scale, group, length, land, queries, c_out, kr_out, state, buf, kr_buf, zero_c, zero_k, in_sem, c_sem, k_sem, ahead):
     first_req, count, first_piece, pieces = group
-    m_ref, l_ref, acc_ref = state
     depth = buf.shape[0]
     rank = buf.shape[3]
     width = kr_buf.shape[1]
     rows = buf.shape[2] * rank // (rank + width)
-    span = rows * HALVES
+    span = rows * PIECES
     steps = count * n
 
     def used(t):
@@ -234,24 +314,10 @@
                 kr_buf[slot, kr_rows, cols] = buf[slot, h, from_rows, from_cols]
         for c in stores(t):
             c.start()
-        qa, qr = queries(t)
-        scores = []
-        for h in range(pieces):
-            s = lax.dot_general(qa, buf[slot, h, :rows, :], (((1,), (1,)), ((), ())), preferred_element_type=jnp.float32)
-            s = s + lax.dot_general(qr, kr_buf[slot, :, h * rows : (h + 1) * rows], (((0,), (0,)), ((), ())), preferred_element_type=jnp.float32)
-            pos = t % n * span + (first_piece + h) * rows + lax.broadcasted_iota(jnp.int32, (1, rows), 1)
-            scores.append(jnp.where(pos < length(req), s * scale, -1e30))
-        m_old = m_ref[...]
-        m_new = m_old
-        for s in scores:
-            m_new = jnp.maximum(m_new, jnp.max(s, axis=-1, keepdims=True))
-        alpha = jnp.exp(m_old - m_new)
-        total, acc = l_ref[...] * alpha, acc_ref[...] * alpha
-        for h, s in enumerate(scores):
-            p = jnp.exp(s - m_new)
-            total = total + jnp.sum(p, axis=-1, keepdims=True)
-            acc = acc + jnp.dot(p.astype(jnp.bfloat16), buf[slot, h, :rows, :], preferred_element_type=jnp.float32)
-        m_ref[...], l_ref[...], acc_ref[...] = m_new, total, acc
+        if queries is not None:
+            qa, qr = queries(t)
+            blocks = [(buf[slot, h, :rows, :], kr_buf[slot, :, h * rows : (h + 1) * rows]) for h in range(pieces)]
+            fold(state, qa, qr, blocks, t % n * span + first_piece * rows, length(req), scale)
 
     def body(t, begin, finish):
         @pl.when(t % n == 0)
@@ -296,14 +362,7 @@
     return run
 
 
-def clear(state):
-    m_ref, l_ref, acc_ref = state
-    m_ref[...] = jnp.full_like(m_ref, -1e30)
-    l_ref[...] = jnp.zeros_like(l_ref)
-    acc_ref[...] = jnp.zeros_like(acc_ref)
-
-
-def first_kernel(n, req_local, scale, lens_ref, land_ref, qa_ref, qr_ref, c_out, kr_out, o_out, part_out,
+def first_kernel(n, req_local, scale, lens_ref, land_ref, qa_ref, qr_ref, o_done, c_out, kr_out, o_out, part_out, o_sem,
                  m_ref, l_ref, acc_ref, part_ref, part_sem, zero_c, zero_k, buf, in_sem, kr_buf, c_sem, k_sem):
     length = lambda m: lens_ref[lax.axis_index("x") * req_local + m]
     zero_c[...] = jnp.zeros_like(zero_c)
@@ -313,8 +372,8 @@
     last = req_local - 1
     rank = acc_ref.shape[1]
 
-    def finish(m):
-        o_out[m] = (acc_ref[...] / l_ref[...]).astype(jnp.bfloat16)
+    done = pltpu.make_async_copy(o_done, o_out.at[pl.ds(0, last)], o_sem)
+    done.start()
 
     def hand_over(m):
         part_ref[:, :rank] = acc_ref[...]
@@ -324,10 +383,11 @@
         copy.start()
         copy.wait()
 
+    piece = lambda m, i: land_ref.at[last, i, pl.ds(0, PIECES - 1)]
+    stream(n, req_local, scale, (last, 1, 0, PIECES - 1), length, piece, lambda t: (qa_ref[last], qr_ref[last]), *rest)(lambda: clear(state), hand_over)
     whole = lambda m, i: land_ref.at[m, i]
-    stream(n, req_local, scale, (0, last, 0, HALVES), length, whole, lambda t: (qa_ref[t // n], qr_ref[t // n]), *rest)(lambda: clear(state), finish)
-    piece = lambda m, i: land_ref.at[last, i, pl.ds(0, HALVES - 1)]
-    stream(n, req_local, scale, (last, 1, 0, HALVES - 1), length, piece, lambda t: (qa_ref[last], qr_ref[last]), *rest)(lambda: clear(state), hand_over)
+    stream(n, req_local, scale, (0, last, 0, PIECES), length, whole, None, *rest)(lambda: None, lambda m: None)
+    done.wait()
 
 
 def last_kernel(n, req_local, scale, lens_ref, land_ref, qa_hbm, qr_hbm, part_hbm, c_old, kr_old, o_old, c_out, kr_out, o_out,
@@ -358,15 +418,15 @@
         copy.start()
         copy.wait()
 
-    stream(n, req_local, scale, (last, 1, HALVES - 1, 1), length, lambda m, i: land_ref.at[i], lambda t: (qa_ref[...], qr_ref[...]), c_out, kr_out, state, buf, kr_buf,
+    stream(n, req_local, scale, (last, 1, PIECES - 1, 1), length, lambda m, i: land_ref.at[pl.ds(i, 1)], lambda t: (qa_ref[...], qr_ref[...]), c_out, kr_out, state, buf, kr_buf,
            zero_c, zero_k, in_sem, c_sem, k_sem, buf.shape[0])(begin, finish)
 
 
-def attend(lens, landed, rest, q_lat, q_rope, n, block):
+def attend(lens, landed, rest, o_done, q_lat, q_rope, n, block):
     req_local, heads, rank = q_lat.shape
     width = q_rope.shape[1]
-    rows = block // HALVES
-    total = rest.shape[2]
+    rows = block // PIECES
+    total = rest.shape[1]
     scale = (rank + width) ** -0.5
     caches = [jax.ShapeDtypeStruct((req_local, n * block, rank), jnp.bfloat16),
               jax.ShapeDtypeStruct((req_local, width, n * block), jnp.bfloat16),
@@ -379,19 +439,19 @@
             pltpu.VMEM((depth, width, pieces * rows), jnp.bfloat16), pltpu.SemaphoreType.DMA((depth, pieces)), pltpu.SemaphoreType.DMA((depth,))]
 
     params = pltpu.CompilerParams(vmem_limit_bytes=ATTEND_BYTES)
-    flops = req_local * n * block * heads * (2 * rank + width) * 2
-    zeros, stores = scratch(n, HALVES)
+    flops = 2 * req_local * n * block * heads * rank
+    zeros, stores = scratch(RING, PIECES)
     *outs, first_part = pl.pallas_call(
         functools.partial(first_kernel, n, req_local, scale),
-        in_specs=[SMEM, HBM, VMEM, VMEM],
-        out_specs=[HBM, HBM, VMEM, HBM],
+        in_specs=[SMEM, HBM, VMEM, VMEM, HBM],
+        out_specs=[HBM] * 4,
         out_shape=caches + [part],
-        scratch_shapes=state + [pltpu.VMEM(part.shape, part.dtype), pltpu.SemaphoreType.DMA] + zeros + [
-            pltpu.VMEM((n, HALVES, total, rank), jnp.bfloat16), pltpu.SemaphoreType.DMA((n,))] + stores,
+        scratch_shapes=[pltpu.SemaphoreType.DMA] + state + [pltpu.VMEM(part.shape, part.dtype), pltpu.SemaphoreType.DMA] + zeros + [
+            pltpu.VMEM((RING, PIECES, total, rank), jnp.bfloat16), pltpu.SemaphoreType.DMA((RING,))] + stores,
         compiler_params=params,
         cost_estimate=pl.CostEstimate(flops=flops, bytes_accessed=req_local * n * block * rank * 4, transcendentals=0),
         name="attend_first",
-    )(lens, landed, q_lat, q_rope)
+    )(lens, landed, q_lat, q_rope, o_done)
     zeros, stores = scratch(n, 1)
     return pl.pallas_call(
         functools.partial(last_kernel, n, req_local, scale),
@@ -403,7 +463,7 @@
             pltpu.VMEM((n, 1, total, rank), jnp.bfloat16), pltpu.SemaphoreType.DMA((n,))] + stores,
         input_output_aliases={5: 0, 6: 1, 7: 2},
         compiler_params=params,
-        cost_estimate=pl.CostEstimate(flops=flops // req_local // HALVES, bytes_accessed=n * block * rank * 2, transcendentals=0),
+        cost_estimate=pl.CostEstimate(flops=flops // req_local // PIECES, bytes_accessed=n * block * rank * 2, transcendentals=0),
         name="attend_last",
     )(lens, rest, q_lat, q_rope, first_part, *outs)
 
@@ -414,9 +474,10 @@
     n = mesh.shape["x"]
 
     def local_step(c_raw, k_raw, norm_gain, rope_cos, rope_sin, seq_lens, q_lat, q_rope):
-        landed, rest = send(seq_lens, c_raw, jnp.swapaxes(k_raw, 1, 2), norm_gain, rope_cos.T, rope_sin.T, n, q_lat.shape[0])
-        rest = lax.all_to_all(rest, "x", 0, 0, tiled=True)[:, None]
-        c_cache, kr_cache, o_lat = attend(seq_lens, landed, rest, q_lat, jnp.swapaxes(q_rope, 1, 2), n, c_raw.shape[1])
+        q_rope = jnp.swapaxes(q_rope, 1, 2)
+        landed, rest, o_done = send(seq_lens, c_raw, jnp.swapaxes(k_raw, 1, 2), norm_gain, rope_cos.T, rope_sin.T, q_lat, q_rope, n)
+        rest = lax.all_to_all(rest, "x", 0, 0, tiled=True)
+        c_cache, kr_cache, o_lat = attend(seq_lens, landed, rest, o_done, q_lat, q_rope, n, c_raw.shape[1])
         return c_cache, jnp.swapaxes(kr_cache, 1, 2), o_lat
 
     return jax.shard_map(local_step, mesh=mesh, in_specs=(seq_spec, seq_spec, P(None), P("x", None), P("x", None), P("dp"), req_spec, req_spec), out_specs=(req_spec, req_spec, req_spec), check_vma=False)

time: 495 us -> 485 us (0.980)
  the two profiles are of different devices: /device:TPU:120 before, /device:TPU:112 now
where the time goes in v4:
time: 485 us; the launch traced here: 483 us
  Pallas kernels  477 us (98%)
    pallas_call x1, Pallas kernels, send(): pl.pallas_call(functools.partial(send_kernel, n, req_local, (rank + width...  440 us
    pallas_call x1, Pallas kernels, attend(): pl.pallas_call(functools.partial(first_kernel, n, req_local, scale), in_s...  29.8 us
  transfers between devices with their start and end apart: 1, of which 0 were waited for; matrix products, arithmetic and copies ran while one was open for 0% of the time, Pallas kernels for 6%

profile of v4, /device:TPU:112, one launch (start us, length us, event | category | flops | bytes accessed | tf_op | source)
XLA Modules:
  0.0 482.6 jit_solution(16107195548378551486)
XLA Ops:
  0.6 440.4 %send.1 = (bf16[6,8,3,288,512]{4,3,2,1,0:T(8,128)(2,1)}, bf16[8,288,512]{2,1,0:T(8,128)(2,1)}, bf16[5,128,512]{2,1,0:T(8,128)(2,1)}) custom-call(s32[48]{0:T(128)} %lens_ref.5, bf16[48,768,512]{2,1,0:T(8,128)(2,1)} %c_hbm.1, bf16[48,64,768]{2,1,0:T(8,128)(2,1)} %bitcast.8, bf16[512]{0:T(512)(128)(2,1)} %gain_ref.1, f32[32,768]{1,0:T(8,128)} %bitcast.10, ...), custom_call_target="tpu_custom_call" | custom-call | flops 1887436800 | bytes 75497472 | tf_op jit(solution)/shard_map/send/pallas_call | solution.py:246
  441.0 0.0 copy-start
  441.0 0.0 copy-start.1
  441.0 0.0 copy-start.2
  441.1 0.0 copy-start.3
  441.1 4.7 all-to-all-start
  445.8 0.0 copy-done
  445.8 0.0 copy-done.1
  445.8 0.0 copy-done.2
  445.8 0.0 copy-done.3
  445.8 29.8 %attend_first.1 = (bf16[6,6144,512]{2,1,0:T(8,128)(2,1)}, bf16[6,64,6144]{2,1,0:T(8,128)(2,1)}, bf16[6,128,512]{2,1,0:T(8,128)(2,1)}, f32[128,768]{1,0:T(8,128)S(1)}) custom-call(s32[48]{0:T(128)S(1)} %copy-done.3, bf16[6,8,3,288,512]{4,3,2,1,0:T(8,128)(2,1)} %get-tuple-element.14.land_ref, bf16[6,128,512]{2,1,0:T(8,128)(2,1)S(1)} %copy-done, ...), custom_call_target="tpu_custom_call" | custom-call | flops 4831838208 | bytes 75497472 | tf_op jit(solution)/shard_map/attend_first/pallas_call | solution.py:444
  475.6 0.0 all-to-all-done.land_ref
  475.6 7.0 %attend_last.1 = (bf16[6,6144,512]{2,1,0:T(8,128)(2,1)}, bf16[6,64,6144]{2,1,0:T(8,128)(2,1)}, bf16[6,128,512]{2,1,0:T(8,128)(2,1)}) custom-call(s32[48]{0:T(128)S(1)} %copy-done.3, bf16[8,288,512]{2,1,0:T(8,128)(2,1)} %all-to-all-done.land_ref, bf16[6,128,512]{2,1,0:T(8,128)(2,1)S(1)} %copy-done, ...), custom_call_target="tpu_custom_call", output_to_operand_aliasing={{0}: (5, {}), {1}: (6, {}), {2}: (7, {})} | custom-call | flops 268435456 | bytes 6291456 | tf_op jit(solution)/shard_map/attend_last/pallas_call | solution.py:456
Async XLA Ops:
  441.0 4.8 copy-start
  441.0 4.8 copy-start.1
  441.0 4.8 copy-start.2
  441.1 4.8 copy-start.3
  441.1 34.6 %all-to-all-start = ((bf16[8,288,512]{2,1,0:T(8,128)(2,1)}), bf16[8,288,512]{2,1,0:T(8,128)(2,1)}, u32[]{:S(2)}, u32[]{:S(2)}) async-start(bf16[8,288,512]{2,1,0:T(8,128)(2,1)} %get-tuple-element.13), calls=%async_computation | async-start | bytes 4718592 | tf_op jit(solution)/shard_map/all_to_all | solution.py:479

commit v5 on v4

--- a/solution.py
+++ b/solution.py
@@ -12,6 +12,7 @@
 ROUNDS = 6
 LOADS = 4
 RING = 12
+BATCH = 4
 AHEAD = 3
 STRIPE = 128
 LANES, SUBLANES = 128, 16
@@ -47,14 +48,14 @@
     acc_ref[...] = jnp.zeros_like(acc_ref)
 
 
-def fold(state, qa, qr, pieces, first, length, scale):
+def fold(state, qa, qr, pieces, firsts, length, scale):
     m_ref, l_ref, acc_ref = state
     scores = []
-    for h, (lat, kr) in enumerate(pieces):
+    for first, (lat, kr) in zip(firsts, pieces):
         s = lax.dot_general(qa, lat, (((1,), (1,)), ((), ())), preferred_element_type=jnp.float32)
         s = s + lax.dot_general(qr, kr, (((0,), (0,)), ((), ())), preferred_element_type=jnp.float32)
         rows = lat.shape[0]
-        pos = first + h * rows + lax.broadcasted_iota(jnp.int32, (1, rows), 1)
+        pos = first + lax.broadcasted_iota(jnp.int32, (1, rows), 1)
         scores.append(jnp.where(pos < length, s * scale, -1e30))
     m_old = m_ref[...]
     m_new = m_old
@@ -219,7 +220,7 @@
             for kr_rows, kr_cols, from_rows, from_cols in rope_tiles(width, rows):
                 kr_buf[kr_rows, kr_cols] = fold_buf[slot, from_rows, from_cols]
             first = (src * PIECES + a // n % PIECES) * rows
-            fold(state, qa_ref[m], qr_ref[m], [(fold_buf[slot, :rows, :], kr_buf[...])], first, lens_ref[me * req_local + m], scale)
+            fold(state, qa_ref[m], qr_ref[m], [(fold_buf[slot, :rows, :], kr_buf[...])], [first], lens_ref[me * req_local + m], scale)
 
             @pl.when(a % per_req == per_req - 1)
             def _():
@@ -317,13 +318,10 @@
         if queries is not None:
             qa, qr = queries(t)
             blocks = [(buf[slot, h, :rows, :], kr_buf[slot, :, h * rows : (h + 1) * rows]) for h in range(pieces)]
-            fold(state, qa, qr, blocks, t % n * span + first_piece * rows, length(req), scale)
-
-    def body(t, begin, finish):
-        @pl.when(t % n == 0)
-        def _():
-            begin()
-
+            firsts = [t % n * span + (first_piece + h) * rows for h in range(pieces)]
+            fold(state, qa, qr, blocks, firsts, length(req), scale)
+
+    def body(t):
         @pl.when(used(t))
         def _():
             work(t)
@@ -342,84 +340,110 @@
 
             fetch(t + ahead)
 
-        @pl.when(t % n == n - 1)
-        def _():
-            finish(first_req + t // n)
-
-    def run(begin, finish):
+    def prologue():
         for t in range(min(ahead, steps)):
             fetch(t)
 
-        @pl.loop(0, steps)
-        def _(t):
-            body(t, begin, finish)
-
+    def drain():
         @pl.loop(max(steps - depth, 0), steps)
         def _(t):
             for c in stores(t):
                 c.wait()
 
-    return run
+    return steps, prologue, body, drain
 
 
 def first_kernel(n, req_local, scale, lens_ref, land_ref, qa_ref, qr_ref, o_done, c_out, kr_out, o_out, part_out, o_sem,
-                 m_ref, l_ref, acc_ref, part_ref, part_sem, zero_c, zero_k, buf, in_sem, kr_buf, c_sem, k_sem):
+                 m_ref, l_ref, acc_ref, part_ref, part_sem, zero_c, zero_k, buf, in_sem, kr_buf, c_sem, k_sem,
+                 side_buf, side_in_sem, side_kr_buf, side_c_sem, side_k_sem):
     length = lambda m: lens_ref[lax.axis_index("x") * req_local + m]
+    state = (m_ref, l_ref, acc_ref)
+    last = req_local - 1
+    rank = acc_ref.shape[1]
+    done = pltpu.make_async_copy(o_done, o_out.at[pl.ds(0, last)], o_sem)
+    piece = lambda m, i: land_ref.at[last, i, pl.ds(0, PIECES - 1)]
+    whole = lambda m, i: land_ref.at[m, i]
+    side_steps, side_prologue, side_body, side_drain = stream(
+        n, req_local, scale, (last, 1, 0, PIECES - 1), length, piece, lambda t: (qa_ref[last], qr_ref[last]), c_out, kr_out, state,
+        side_buf, side_kr_buf, zero_c, zero_k, side_in_sem, side_c_sem, side_k_sem, n)
+    steps, prologue, body, drain = stream(
+        n, req_local, scale, (0, last, 0, PIECES), length, whole, None, c_out, kr_out, state,
+        buf, kr_buf, zero_c, zero_k, in_sem, c_sem, k_sem, buf.shape[0] // 2)
+
+    side_prologue()
+    prologue()
+    done.start()
     zero_c[...] = jnp.zeros_like(zero_c)
     zero_k[...] = jnp.zeros_like(zero_k)
-    state = (m_ref, l_ref, acc_ref)
-    rest = (c_out, kr_out, state, buf, kr_buf, zero_c, zero_k, in_sem, c_sem, k_sem, buf.shape[0] // 2)
+    clear(state)
+    every = steps // side_steps
+
+    @pl.loop(0, steps)
+    def _(t):
+        body(t)
+
+        @pl.when(t % every == 0)
+        def _():
+            side_body(t // every)
+
+    part_ref[:, :rank] = acc_ref[...]
+    part_ref[:, rank : rank + LANES] = jnp.broadcast_to(m_ref[...], (part_ref.shape[0], LANES))
+    part_ref[:, rank + LANES :] = jnp.broadcast_to(l_ref[...], (part_ref.shape[0], LANES))
+    copy = pltpu.make_async_copy(part_ref, part_out, part_sem)
+    copy.start()
+    copy.wait()
+    drain()
+    side_drain()
+    done.wait()
+
+
+def last_kernel(n, req_local, scale, lens_ref, land_ref, qa_hbm, qr_hbm, part_hbm, c_old, kr_old, o_old, c_out, kr_out, o_out,
+                m_ref, l_ref, acc_ref, qa_ref, qr_ref, part_ref, o_buf, sems, buf, in_sem, kr_buf, c_sem, k_sem):
     last = req_local - 1
-    rank = acc_ref.shape[1]
-
-    done = pltpu.make_async_copy(o_done, o_out.at[pl.ds(0, last)], o_sem)
-    done.start()
-
-    def hand_over(m):
-        part_ref[:, :rank] = acc_ref[...]
-        part_ref[:, rank : rank + LANES] = jnp.broadcast_to(m_ref[...], (part_ref.shape[0], LANES))
-        part_ref[:, rank + LANES :] = jnp.broadcast_to(l_ref[...], (part_ref.shape[0], LANES))
-        copy = pltpu.make_async_copy(part_ref, part_out, part_sem)
-        copy.start()
-        copy.wait()
-
-    piece = lambda m, i: land_ref.at[last, i, pl.ds(0, PIECES - 1)]
-    stream(n, req_local, scale, (last, 1, 0, PIECES - 1), length, piece, lambda t: (qa_ref[last], qr_ref[last]), *rest)(lambda: clear(state), hand_over)
-    whole = lambda m, i: land_ref.at[m, i]
-    stream(n, req_local, scale, (0, last, 0, PIECES), length, whole, None, *rest)(lambda: None, lambda m: None)
-    done.wait()
-
-
-def last_kernel(n, req_local, scale, lens_ref, land_ref, qa_hbm, qr_hbm, part_hbm, c_old, kr_old, o_old, c_out, kr_out, o_out,
-                m_ref, l_ref, acc_ref, qa_ref, qr_ref, part_ref, o_buf, sems, zero_c, zero_k, buf, in_sem, kr_buf, c_sem, k_sem):
-    length = lambda m: lens_ref[lax.axis_index("x") * req_local + m]
-    last = req_local - 1
+    length = lens_ref[lax.axis_index("x") * req_local + last]
     state = (m_ref, l_ref, acc_ref)
     rank = acc_ref.shape[1]
+    width = kr_buf.shape[1]
+    rows = kr_buf.shape[2]
+    block = rows * PIECES
+    loads = [pltpu.make_async_copy(land_ref.at[i], buf.at[i], in_sem.at[i]) for i in range(n)]
+    for c in loads:
+        c.start()
     copies = [pltpu.make_async_copy(qa_hbm.at[last], qa_ref, sems.at[0]), pltpu.make_async_copy(qr_hbm.at[last], qr_ref, sems.at[1]),
               pltpu.make_async_copy(part_hbm, part_ref, sems.at[2])]
     for c in copies:
         c.start()
-    zero_c[...] = jnp.zeros_like(zero_c)
-    zero_k[...] = jnp.zeros_like(zero_k)
-
-    def begin():
-        clear(state)
-        for c in copies:
-            c.wait()
-
-    def finish(m):
-        m_part, l_part, acc_part = part_ref[:, rank : rank + 1], part_ref[:, rank + LANES : rank + LANES + 1], part_ref[:, :rank]
-        m_new = jnp.maximum(m_ref[...], m_part)
-        here, there = jnp.exp(m_ref[...] - m_new), jnp.exp(m_part - m_new)
-        total = l_ref[...] * here + l_part * there
-        o_buf[...] = ((acc_ref[...] * here + acc_part * there) / total).astype(jnp.bfloat16)
-        copy = pltpu.make_async_copy(o_buf, o_out.at[m], sems.at[3])
-        copy.start()
-        copy.wait()
-
-    stream(n, req_local, scale, (last, 1, PIECES - 1, 1), length, lambda m, i: land_ref.at[pl.ds(i, 1)], lambda t: (qa_ref[...], qr_ref[...]), c_out, kr_out, state, buf, kr_buf,
-           zero_c, zero_k, in_sem, c_sem, k_sem, buf.shape[0])(begin, finish)
+    clear(state)
+    stores = []
+    for at in range(0, n, BATCH):
+        batch = range(at, at + BATCH)
+        for i in batch:
+            first = i * block + block - rows
+            loads[i].wait()
+            stores.append(pltpu.make_async_copy(buf.at[i, pl.ds(0, rows), :], c_out.at[last, pl.ds(first, rows), :], c_sem.at[i]))
+            stores[-1].start()
+            for kr_rows, kr_cols, from_rows, from_cols in rope_tiles(width, rows):
+                kr_buf[i, kr_rows, kr_cols] = buf[i, from_rows, from_cols]
+            stores.append(pltpu.make_async_copy(kr_buf.at[i], kr_out.at[last, :, pl.ds(first, rows)], k_sem.at[i]))
+            stores[-1].start()
+        if at == 0:
+            for c in copies:
+                c.wait()
+
+        @pl.when(at * block + block - rows < length)
+        def _():
+            blocks = [(buf[i, :rows, :], kr_buf[i]) for i in batch]
+            fold(state, qa_ref[...], qr_ref[...], blocks, [i * block + block - rows for i in batch], length, scale)
+
+    m_part, l_part, acc_part = part_ref[:, rank : rank + 1], part_ref[:, rank + LANES : rank + LANES + 1], part_ref[:, :rank]
+    m_new = jnp.maximum(m_ref[...], m_part)
+    here, there = jnp.exp(m_ref[...] - m_new), jnp.exp(m_part - m_new)
+    total = l_ref[...] * here + l_part * there
+    o_buf[...] = ((acc_ref[...] * here + acc_part * there) / total).astype(jnp.bfloat16)
+    copy = pltpu.make_async_copy(o_buf, o_out.at[last], sems.at[3])
+    copy.start()
+    for c in stores + [copy]:
+        c.wait()
 
 
 def attend(lens, landed, rest, o_done, q_lat, q_rope, n, block):
@@ -434,33 +458,32 @@
     part = jax.ShapeDtypeStruct((heads, rank + 2 * LANES), jnp.float32)
     state = [pltpu.VMEM((heads, 1), jnp.float32), pltpu.VMEM((heads, 1), jnp.float32), pltpu.VMEM((heads, rank), jnp.float32)]
 
-    def scratch(depth, pieces):
-        return [pltpu.VMEM((rows, rank), jnp.bfloat16), pltpu.VMEM((width, pieces * rows), jnp.bfloat16)], [
-            pltpu.VMEM((depth, width, pieces * rows), jnp.bfloat16), pltpu.SemaphoreType.DMA((depth, pieces)), pltpu.SemaphoreType.DMA((depth,))]
+    def ring(depth, *pieces):
+        count = pieces[0] if pieces else 1
+        return [pltpu.VMEM((depth, *pieces, total, rank), jnp.bfloat16), pltpu.SemaphoreType.DMA((depth,)),
+                pltpu.VMEM((depth, width, count * rows), jnp.bfloat16), pltpu.SemaphoreType.DMA((depth, *pieces)), pltpu.SemaphoreType.DMA((depth,))]
 
     params = pltpu.CompilerParams(vmem_limit_bytes=ATTEND_BYTES)
     flops = 2 * req_local * n * block * heads * rank
-    zeros, stores = scratch(RING, PIECES)
     *outs, first_part = pl.pallas_call(
         functools.partial(first_kernel, n, req_local, scale),
         in_specs=[SMEM, HBM, VMEM, VMEM, HBM],
         out_specs=[HBM] * 4,
         out_shape=caches + [part],
-        scratch_shapes=[pltpu.SemaphoreType.DMA] + state + [pltpu.VMEM(part.shape, part.dtype), pltpu.SemaphoreType.DMA] + zeros + [
-            pltpu.VMEM((RING, PIECES, total, rank), jnp.bfloat16), pltpu.SemaphoreType.DMA((RING,))] + stores,
+        scratch_shapes=[pltpu.SemaphoreType.DMA] + state + [pltpu.VMEM(part.shape, part.dtype), pltpu.SemaphoreType.DMA,
+                                                            pltpu.VMEM((rows, rank), jnp.bfloat16), pltpu.VMEM((width, block), jnp.bfloat16)]
+        + ring(RING, PIECES) + ring(n, PIECES - 1),
         compiler_params=params,
         cost_estimate=pl.CostEstimate(flops=flops, bytes_accessed=req_local * n * block * rank * 4, transcendentals=0),
         name="attend_first",
     )(lens, landed, q_lat, q_rope, o_done)
-    zeros, stores = scratch(n, 1)
     return pl.pallas_call(
         functools.partial(last_kernel, n, req_local, scale),
         in_specs=[SMEM] + [HBM] * 7,
         out_specs=[HBM] * 3,
         out_shape=caches,
         scratch_shapes=state + [pltpu.VMEM((heads, rank), jnp.bfloat16), pltpu.VMEM((width, heads), jnp.bfloat16), pltpu.VMEM(part.shape, part.dtype),
-                                pltpu.VMEM((heads, rank), jnp.bfloat16), pltpu.SemaphoreType.DMA((4,))] + zeros + [
-            pltpu.VMEM((n, 1, total, rank), jnp.bfloat16), pltpu.SemaphoreType.DMA((n,))] + stores,
+                                pltpu.VMEM((heads, rank), jnp.bfloat16), pltpu.SemaphoreType.DMA((4,))] + ring(n),
         input_output_aliases={5: 0, 6: 1, 7: 2},
         compiler_params=params,
         cost_estimate=pl.CostEstimate(flops=flops // req_local // PIECES, bytes_accessed=n * block * rank * 2, transcendentals=0),

time: 485 us -> 480 us (0.990)
  Pallas kernels: 477 us -> 470 us
  waiting for transfers between devices: 0.01 us -> 5.17 us
    pallas_call x1, Pallas kernels: 29.8 us -> 24.6 us  [attend(): pl.pallas_call(functools.partial(first_kernel, n, req_local, scale), in_s...]
    all_to_all x1, waiting for transfers between devices: 0.01 us -> 5.17 us  [local_step(): rest = lax.all_to_all(rest, 'x', 0, 0, tiled=True)]
  transfers between devices with their start and end apart: 1 -> 1, of which waited for: 0 -> 1; matrix products, arithmetic and copies ran while one was open for 0% -> 0% of each run, Pallas kernels for 6% -> 5%
where the time goes in v5:
time: 480 us
  Pallas kernels  470 us (98%)
  waiting for transfers between devices  5.17 us (1%)
    pallas_call x1, Pallas kernels, send(): pl.pallas_call(functools.partial(send_kernel, n, req_local, (rank + width...  440 us
    pallas_call x1, Pallas kernels, attend(): pl.pallas_call(functools.partial(first_kernel, n, req_local, scale), in_s...  24.6 us
  transfers between devices with their start and end apart: 1, of which 1 were waited for; matrix products, arithmetic and copies ran while one was open for 0% of the time, Pallas kernels for 5%

profile of v5, /device:TPU:112, one launch (start us, length us, event | category | flops | bytes accessed | tf_op | source)
XLA Modules:
  0.0 480.4 jit_solution(3690160376807237190)
XLA Ops:
  0.6 440.4 %send.1 = (bf16[6,8,3,288,512]{4,3,2,1,0:T(8,128)(2,1)}, bf16[8,288,512]{2,1,0:T(8,128)(2,1)}, bf16[5,128,512]{2,1,0:T(8,128)(2,1)}) custom-call(s32[48]{0:T(128)} %lens_ref.5, bf16[48,768,512]{2,1,0:T(8,128)(2,1)} %c_hbm.1, bf16[48,64,768]{2,1,0:T(8,128)(2,1)} %bitcast.8, bf16[512]{0:T(512)(128)(2,1)} %gain_ref.1, f32[32,768]{1,0:T(8,128)} %bitcast.10, ...), custom_call_target="tpu_custom_call" | custom-call | flops 1887436800 | bytes 75497472 | tf_op jit(solution)/shard_map/send/pallas_call | solution.py:247
  441.0 0.0 copy-start
  441.0 0.0 copy-start.1
  441.0 0.0 copy-start.2
  441.1 0.0 copy-start.3
  441.1 4.7 all-to-all-start
  445.8 0.0 copy-done
  445.8 0.0 copy-done.1
  445.8 0.0 copy-done.2
  445.8 0.0 copy-done.3
  445.8 24.6 %attend_first.1 = (bf16[6,6144,512]{2,1,0:T(8,128)(2,1)}, bf16[6,64,6144]{2,1,0:T(8,128)(2,1)}, bf16[6,128,512]{2,1,0:T(8,128)(2,1)}, f32[128,768]{1,0:T(8,128)S(1)}) custom-call(s32[48]{0:T(128)S(1)} %copy-done.3, bf16[6,8,3,288,512]{4,3,2,1,0:T(8,128)(2,1)} %get-tuple-element.14.land_ref, bf16[6,128,512]{2,1,0:T(8,128)(2,1)S(1)} %copy-done, ...), custom_call_target="tpu_custom_call" | custom-call | flops 4831838208 | bytes 75497472 | tf_op jit(solution)/shard_map/attend_first/pallas_call | solution.py:468
  470.4 5.2 %all-to-all-done.land_ref = bf16[8,288,512]{2,1,0:T(8,128)(2,1)} async-done(((bf16[8,288,512]{2,1,0:T(8,128)(2,1)}), bf16[8,288,512]{2,1,0:T(8,128)(2,1)}, u32[]{:S(2)}, u32[]{:S(2)}) %all-to-all-start) | async-done | bytes 2359328 | tf_op jit(solution)/shard_map/all_to_all | solution.py:502
  475.6 4.8 %attend_last.1 = (bf16[6,6144,512]{2,1,0:T(8,128)(2,1)}, bf16[6,64,6144]{2,1,0:T(8,128)(2,1)}, bf16[6,128,512]{2,1,0:T(8,128)(2,1)}) custom-call(s32[48]{0:T(128)S(1)} %copy-done.3, bf16[8,288,512]{2,1,0:T(8,128)(2,1)} %all-to-all-done.land_ref, bf16[6,128,512]{2,1,0:T(8,128)(2,1)S(1)} %copy-done, ...), custom_call_target="tpu_custom_call", output_to_operand_aliasing={{0}: (5, {}), {1}: (6, {}), {2}: (7, {})} | custom-call | flops 268435456 | bytes 6291456 | tf_op jit(solution)/shard_map/attend_last/pallas_call | solution.py:480
Async XLA Ops:
  441.0 4.8 copy-start
  441.0 4.8 copy-start.1
  441.0 4.8 copy-start.2
  441.1 4.8 copy-start.3
  441.1 34.5 %all-to-all-start = ((bf16[8,288,512]{2,1,0:T(8,128)(2,1)}), bf16[8,288,512]{2,1,0:T(8,128)(2,1)}, u32[]{:S(2)}, u32[]{:S(2)}) async-start(bf16[8,288,512]{2,1,0:T(8,128)(2,1)} %get-tuple-element.13), calls=%async_computation | async-start | bytes 4718592 | tf_op jit(solution)/shard_map/all_to_all | solution.py:502
